TPU v7x, 32 devices: a whole 2x2x4 slice. The times are simulated.
32 devices in a mesh: rep: 1, dp: 32 (over x, y, z, core).
Axes of the slice: x: 2, y: 2, z: 4, core: 2. Of those that a mesh axis runs over, the one named last changes fastest.
Arguments:
- x: bfloat16 [32, 2048, 1024], P(('rep', 'dp'))
- dy: bfloat16 [32, 2048, 1024], P(('rep', 'dp'))
- w_gate: bfloat16 [2, 1024, 5120], replicated
- w_up: bfloat16 [2, 1024, 5120], replicated
- w_down: bfloat16 [2, 5120, 1024], replicated
- m_w_gate: float32 [2, 1024, 5120], P(None, 'dp')
- m_w_up: float32 [2, 1024, 5120], P(None, 'dp')
- m_w_down: float32 [2, 5120, 1024], P(None, 'dp')
- v_w_gate: float32 [2, 1024, 5120], P(None, 'dp')
- v_w_up: float32 [2, 1024, 5120], P(None, 'dp')
- v_w_down: float32 [2, 5120, 1024], P(None, 'dp')
Outputs:
- output 1: bfloat16 [2, 1024, 5120], P('rep')
- output 2: bfloat16 [2, 1024, 5120], P('rep')
- output 3: bfloat16 [2, 5120, 1024], P('rep')
- output 4: float32 [2, 1024, 5120], P('rep', 'dp')
- output 5: float32 [2, 1024, 5120], P('rep', 'dp')
- output 6: float32 [2, 5120, 1024], P('rep', 'dp')
- output 7: float32 [2, 1024, 5120], P('rep', 'dp')
- output 8: float32 [2, 1024, 5120], P('rep', 'dp')
- output 9: float32 [2, 5120, 1024], P('rep', 'dp')
All inputs are finite; a program needn't handle non-finite values.
Results may differ from a plain program's by a relative error of at most 0.022.
Values are sent between devices in bfloat16 or wider.
A program may use at most 2 GiB of HBM per device.

v0:
```python
import jax
import jax.numpy as jnp
from jax import lax

NAMES = ("w_gate", "w_up", "w_down")


def matmul(a, w):
    return jnp.dot(a, w, preferred_element_type=jnp.float32).astype(jnp.bfloat16)


def normed(h):
    wide = h.astype(jnp.float32)
    scale = lax.rsqrt(jnp.mean(wide**2, -1, keepdims=True) + 1e-6)
    return (wide * scale).astype(jnp.bfloat16)


def layer(h, w):
    a = normed(h)
    gate = jnp.dot(a, w["w_gate"], preferred_element_type=jnp.float32)
    up = jnp.dot(a, w["w_up"], preferred_element_type=jnp.float32)
    return h + matmul((jax.nn.silu(gate) * up).astype(jnp.bfloat16), w["w_down"])


def adamw(w, m, v, g):
    m = 0.9 * m + 0.1 * g
    v = 0.95 * v + 0.05 * g * g
    step = m * lax.rsqrt(v + 1e-8) + 0.1 * w
    return (w - 0.02 * step).astype(jnp.bfloat16), m, v


def stack(weights, h):
    for number in range(weights["w_gate"].shape[0]):
        h = layer(h, {name: w[number] for name, w in weights.items()})
    return h


def solution(mesh):
    groups = mesh.shape["rep"]

    def step(x, dy, *arrays):
        weights, m, v = (arrays[i : i + 3] for i in (0, 3, 6))
        x, dy = (t.reshape(groups, -1, *t.shape[1:]) for t in (x, dy))

        def of_a_group(x, dy):
            _, back = jax.vjp(lambda w: stack(w, x), dict(zip(NAMES, weights, strict=True)))
            by_weights = back(dy)[0]
            gradients = [by_weights[name].astype(jnp.float32) for name in NAMES]
            new = [adamw(w.astype(jnp.float32), m, v, g) for w, m, v, g in zip(weights, m, v, gradients, strict=True)]
            return tuple(one[which] for which in range(3) for one in new)

        return tuple(t.reshape(-1, *t.shape[2:]) for t in jax.vmap(of_a_group)(x, dy))

    return step
```

profile of v0, /device:TPU:0, one launch (start us, length us, event | category | flops | bytes accessed | tf_op | source)
XLA Modules:
  0.0 2908.8 jit_solution(12406604756619391559)
XLA Ops:
  20.3 29.0 fusion.166
  49.3 50.3 %fusion.150 = (bf16[1,2048,5120]{2,1,0:T(8,128)(2,1)}, f32[2048,5120]{1,0:T(8,128)}) fusion(f32[2048,5120]{1,0:T(8,128)} %fusion.166, bf16[2,1024,5120]{2,1,0:T(8,128)(2,1)} %param.17, bf16[1,2048,1024]{1,2,0:T(8,128)(2,1)} %copy-done.4), kind=kOutput, calls=%fused_computation.189 | convolution fusion | flops 21537751040 | bytes 119537664 | tf_op jit(solution)/vmap(jvp())/dot_general | solution.py:21
  99.6 29.9 %fusion.182 = (f32[2048]{0:T(1024)S(1)}, bf16[1,2048,1024]{1,2,0:T(8,128)(2,1)}) fusion(bf16[1,2048,1024]{1,2,0:T(8,128)(2,1)} %copy.1, bf16[2,5120,1024]{2,1,0:T(8,128)(2,1)} %param.15, bf16[1,2048,5120]{2,1,0:T(8,128)(2,1)} %get-tuple-element.263), kind=kOutput, calls=%fused_computation.233 | convolution fusion | flops 21485320192 | bytes 39854080 | tf_op jit(solution)/vmap(jvp())/dot_general | solution.py:9
  135.5 29.1 fusion.156
  164.6 50.7 %fusion.149 = (bf16[1,2048,5120]{2,1,0:T(8,128)(2,1)}, f32[2048,5120]{1,0:T(8,128)}) fusion(f32[2048,5120]{1,0:T(8,128)} %fusion.156, bf16[2,1024,5120]{2,1,0:T(8,128)(2,1)} %param.17, bf16[1,2048,1024]{1,2,0:T(8,128)(2,1)} %copy-done.7), kind=kOutput, calls=%fused_computation.187 | convolution fusion | flops 21537751040 | bytes 119537664 | tf_op jit(solution)/vmap(jvp())/dot_general | solution.py:21
  215.2 28.3 copy.3
  243.5 341.1 %while.16 = (bf16[1,2048,5120]{1,2,0:T(8,128)(2,1)}, bf16[1,2048,1024]{2,1,0:T(8,128)(2,1)}, f32[160,1024]{1,0:T(8,128)S(1)}, f32[160,1024]{1,0:T(8,128)}, u32[]...) while((bf16[1,2048,5120]{1,2,0:T(8,128)(2,1)}, ...), condition=%wide.windowed_dot_general_cond_rs.4.clone, body=%wide.windowed_dot_general_body_rs.4.clone.sunk | while | flops 2690580480 | bytes 73925192 | solution.py:9
  293.6 10.5 collective-permute-done.16
  335.3 10.2 collective-permute-done.16
  355.3 10.8 collective-permute-done.18
  378.0 10.6 collective-permute-done.16
  398.4 11.0 collective-permute-done.18
  421.2 11.0 collective-permute-done.16
  442.0 11.0 collective-permute-done.18
  464.7 11.0 collective-permute-done.16
  485.5 11.0 collective-permute-done.18
  508.3 11.0 collective-permute-done.16
  529.1 11.0 collective-permute-done.18
  551.8 11.0 collective-permute-done.16
  572.6 11.0 collective-permute-done.18
  591.4 28.2 copy.5
  619.6 55.9 %convert_multiply_fusion.2 = (bf16[1,2048,5120]{2,1,0:T(8,128)(2,1)}, bf16[1,2048,5120]{2,1,0:T(8,128)(2,1)}) fusion(f32[2048,5120]{1,0:T(8,128)} %fusion.156, f32[2048,5120]{1,0:T(8,128)} %get-tuple-element.270, bf16[2,5120,1024]{2,1,0:T(8,128)(2,1)} %param.15, bf16[1,2048,1024]{2,1,0:T(8,128)(2,1)} %get-tuple-element.744), kind=kOutput, calls=%fused_computation.170 | convolution fusion | flops 21642608640 | bytes 140509184 | tf_op jit(solution)/vmap(transpose(jvp()))/dot_general | solution.py:9
  675.5 29.2 %fusion.142 = bf16[2048,1024]{0,1:T(8,128)(2,1)} fusion(bf16[1,2048,5120]{2,1,0:T(8,128)(2,1)} %get-tuple-element.541, bf16[2,1024,5120]{2,1,0:T(8,128)(2,1)} %param.12), kind=kOutput, calls=%fused_computation.176 | convolution fusion | flops 21474836480 | bytes 35651584 | tf_op jit(solution)/vmap(transpose(jvp()))/dot_general | solution.py:20
  704.8 30.4 %fusion.184 = (f32[2048]{0:T(1024)S(1)}, bf16[2048,1024]{0,1:T(8,128)(2,1)}) fusion(bf16[1,2048,1024]{1,2,0:T(8,128)(2,1)S(1)} %copy-done.21, bf16[2048,1024]{0,1:T(8,128)(2,1)} %fusion.142, bf16[2,1024,5120]{2,1,0:T(8,128)(2,1)} %param.17, bf16[1,2048,5120]{2,1,0:T(8,128)(2,1)} %get-tuple-element.613), kind=kOutput, calls=%fused_computation.235 | convolution fusion | flops 21485320192 | bytes 44048384 | tf_op jit(solution)/vmap(transpose(jvp()))/dot_general | solution.py:21
  748.4 344.8 %while.17 = (bf16[1,2048,1024]{2,1,0:T(8,128)(2,1)}, bf16[1,2048,5120]{1,2,0:T(8,128)(2,1)}, f32[1024,160]{0,1:T(8,128)S(1)}, f32[1024,160]{0,1:T(8,128)}, u32[]...) while((bf16[1,2048,1024]{2,1,0:T(8,128)(2,1)}, ...), condition=%wide.windowed_dot_general_cond_rs.5.clone, body=%wide.windowed_dot_general_body_rs.5.clone.sunk | while | flops 2690580480 | bytes 73925192 | solution.py:9
  778.1 10.4 collective-permute-done.22
  800.4 10.2 collective-permute-done.20
  820.4 10.7 collective-permute-done.22
  842.9 10.7 collective-permute-done.20
  863.3 11.1 collective-permute-done.22
  886.2 11.0 collective-permute-done.20
  907.0 10.9 collective-permute-done.22
  929.8 10.9 collective-permute-done.20
  950.5 11.0 collective-permute-done.22
  973.3 11.0 collective-permute-done.20
  994.1 10.9 collective-permute-done.22
  1016.9 10.9 collective-permute-done.20
  1037.6 11.0 collective-permute-done.22
  1060.4 11.0 collective-permute-done.20
  1081.2 10.9 collective-permute-done.22
  1094.1 360.3 %while.14 = (bf16[1,2048,5120]{2,1,0:T(8,128)(2,1)}, bf16[1,2048,1024]{1,2,0:T(8,128)(2,1)}, f32[5120,32]{0,1:T(8,128)S(1)}, f32[5120,32]{0,1:T(8,128)}, u32[]{:...) while((bf16[1,2048,5120]{2,1,0:T(8,128)(2,1)}, ...), condition=%wide.windowed_dot_general_cond_rs.2.clone, body=%wide.windowed_dot_general_body_rs.2.clone.sunk | while | flops 2686386176 | bytes 174588576 | solution.py:21
  1109.0 12.2 collective-permute-done.8
  1455.3 55.3 %convert_multiply_fusion = (bf16[1,2048,5120]{2,1,0:T(8,128)(2,1)}, bf16[1,2048,5120]{2,1,0:T(8,128)(2,1)}) fusion(f32[2048,5120]{1,0:T(8,128)} %fusion.166, f32[2048,5120]{1,0:T(8,128)} %get-tuple-element.264, bf16[2,5120,1024]{2,1,0:T(8,128)(2,1)} %param.15, bf16[1,2048,1024]{1,2,0:T(8,128)(2,1)} %fusion.185), kind=kOutput, calls=%fused_computation.168 | convolution fusion | flops 21642608640 | bytes 140509184 | tf_op jit(solution)/vmap(transpose(jvp()))/dot_general | solution.py:9
  1510.6 349.7 %while.15 = (bf16[1,2048,5120]{2,1,0:T(8,128)(2,1)}, bf16[1,2048,1024]{1,2,0:T(8,128)(2,1)}, f32[5120,32]{0,1:T(8,128)S(1)}, f32[5120,32]{0,1:T(8,128)}, u32[]{:...) while((bf16[1,2048,5120]{2,1,0:T(8,128)(2,1)}, ...), condition=%wide.windowed_dot_general_cond_rs.3.clone, body=%wide.windowed_dot_general_body_rs.3.clone.sunk | while | flops 2686386176 | bytes 177210048 | solution.py:21
  1541.4 11.0 collective-permute-done.14
  1847.2 10.0 collective-permute-done.14
  1868.0 410.4 %while.12 = (bf16[1,2048,5120]{2,1,0:T(8,128)(2,1)}, bf16[1,2048,1024]{1,2,0:T(8,128)(2,1)}, f32[5120,32]{0,1:T(8,128)S(1)}, f32[5120,32]{0,1:T(8,128)}, u32[]{:...) while((bf16[1,2048,5120]{2,1,0:T(8,128)(2,1)}, ...), condition=%wide.windowed_dot_general_cond_rs.clone, body=%wide.windowed_dot_general_body_rs.clone.sunk | while | flops 2686386176 | bytes 177210048 | solution.py:20
  1899.4 22.6 collective-permute-done.2
  1941.7 17.1 collective-permute-done
  1970.1 15.6 collective-permute-done.2
  2005.4 17.8 collective-permute-done
  2036.0 22.3 collective-permute-done.2
  2178.5 10.3 collective-permute-done.2
  2285.3 427.0 %while.13 = (bf16[1,2048,5120]{2,1,0:T(8,128)(2,1)}, bf16[1,2048,1024]{1,2,0:T(8,128)(2,1)}, f32[5120,32]{0,1:T(8,128)S(1)}, f32[5120,32]{0,1:T(8,128)}, u32[]{:...) while((bf16[1,2048,5120]{2,1,0:T(8,128)(2,1)}, ...), condition=%wide.windowed_dot_general_cond_rs.1.clone, body=%wide.windowed_dot_general_body_rs.1.clone.sunk | while | flops 2686386176 | bytes 177210048 | solution.py:20
  2316.1 23.1 collective-permute-done.6
  2358.8 17.2 collective-permute-done.4
  2387.7 17.0 collective-permute-done.6
  2424.4 19.1 collective-permute-done.4
  2445.6 29.6 %collective-permute-start.6 = (f32[5120,32]{0,1:T(8,128)}, f32[5120,32]{0,1:T(8,128)S(1)}, u32[]{:S(2)}, u32[]{:S(2)}) collective-permute-start(f32[5120,32]{0,1:T(8,128)} %get-tuple-element.465), channel_id=11, source_target_pairs={{0,1},{1,2},{2,3},{3,4},{4,5},{5,6},{6,7},{7,8},{8,9},{9,10},{10,1... | collective-permute-start | bytes 1966088 | tf_op jit(solution)/vmap(transpose(jvp()))/dot_general | solution.py:20
  2525.3 10.8 collective-permute-done.6
  2713.4 12.4 collective-permute-done.25
  2730.3 129.5 %all-gather.10.cloned.1.call-done = bf16[1,2,1024,5120]{3,2,1,0:T(8,128)(2,1)} async-done(((bf16[1,2,32,5120]{3,2,1,0:T(8,128)(2,1)}), bf16[1,2,1024,5120]{3,2,1,0:T(8,128)(2,1)}) %all-gather.10.cloned.1.call-update) | async-done | bytes 20971536 | tf_op jit(solution)/reshape | solution.py:52
  2859.8 20.9 copy.63
  2880.8 10.6 copy.64
  (904 shorter events, 1742.5 us)
Async XLA Ops:
  7.2 2723.1 %all-gather.14.cloned.1.call-start = ((), (), s32[]{:S(2)}) async-start(), calls=%async_computation.2 | async-start | bytes 21626880 | tf_op jit(solution)/reshape | solution.py:52
  388.8 20.5 collective-permute-start.18
  388.9 20.5 collective-permute-start.19
  411.6 20.6 collective-permute-start.16
  411.7 20.5 collective-permute-start.17
  432.4 20.5 collective-permute-start.18
  455.1 20.6 collective-permute-start.16
  455.2 20.5 collective-permute-start.17
  475.9 20.5 collective-permute-start.18
  476.0 20.5 collective-permute-start.19
  498.7 20.6 collective-permute-start.16
  498.8 20.5 collective-permute-start.17
  519.6 20.5 collective-permute-start.18
  542.2 20.6 collective-permute-start.16
  542.4 20.5 collective-permute-start.17
  563.1 20.5 collective-permute-start.18
  563.1 20.5 collective-permute-start.19
  584.6 1276.5 %collective-permute-start.28 = (f32[160,1024]{1,0:T(8,128)}, f32[160,1024]{1,0:T(8,128)}, u32[]{:S(2)}, u32[]{:S(2)}) collective-permute-start(f32[160,1024]{1,0:T(8,128)} %get-tuple-element.45), channel_id=32, source_target_pairs={{0,1},{1,2},{2,3},{3,4},{4,5},{5,6},{6,7},{7,8},{8,9},{9,10},{10,1... | collective-permute-start | bytes 1966088 | tf_op jit(solution)/vmap(transpose(jvp()))/dot_general | solution.py:9
  853.8 20.6 collective-permute-start.22
  853.9 20.5 collective-permute-start.23
  876.6 20.7 collective-permute-start.20
  876.7 20.5 collective-permute-start.21
  897.5 20.4 collective-permute-start.22
  920.1 20.6 collective-permute-start.20
  940.9 20.5 collective-permute-start.22
  941.0 20.5 collective-permute-start.23
  963.7 20.7 collective-permute-start.20
  963.8 20.5 collective-permute-start.21
  1007.2 20.6 collective-permute-start.20
  1028.1 20.5 collective-permute-start.22
  1028.1 20.5 collective-permute-start.23
  1050.8 20.7 collective-permute-start.20
  1050.9 20.5 collective-permute-start.21
  1071.7 20.4 collective-permute-start.22
  1093.3 769.1 %collective-permute-start.29 = (f32[1024,160]{0,1:T(8,128)}, f32[1024,160]{0,1:T(8,128)}, u32[]{:S(2)}, u32[]{:S(2)}) collective-permute-start(f32[1024,160]{0,1:T(8,128)} %get-tuple-element.47), channel_id=38, source_target_pairs={{0,1},{1,2},{2,3},{3,4},{4,5},{5,6},{6,7},{7,8},{8,9},{9,10},{10,1... | collective-permute-start | bytes 1966088 | tf_op jit(solution)/vmap(transpose(jvp()))/dot_general | solution.py:9
  1094.2 27.0 collective-permute-start.8
  1094.3 26.9 collective-permute-start.9
  1455.3 823.1 %collective-permute-start.26 = (f32[5120,32]{0,1:T(8,128)}, f32[5120,32]{0,1:T(8,128)}, u32[]{:S(2)}, u32[]{:S(2)}) collective-permute-start(f32[5120,32]{0,1:T(8,128)} %get-tuple-element.41), channel_id=19, source_target_pairs={{0,1},{1,2},{2,3},{3,4},{4,5},{5,6},{6,7},{7,8},{8,9},{9,10},{10,1... | collective-permute-start | bytes 1966088 | tf_op jit(solution)/vmap(transpose(jvp()))/dot_general | solution.py:21
  1532.3 21.0 collective-permute-start.15
  1860.3 419.4 %collective-permute-start.27 = (f32[5120,32]{0,1:T(8,128)}, f32[5120,32]{0,1:T(8,128)}, u32[]{:S(2)}, u32[]{:S(2)}) collective-permute-start(f32[5120,32]{0,1:T(8,128)} %get-tuple-element.43), channel_id=25, source_target_pairs={{0,1},{1,2},{2,3},{3,4},{4,5},{5,6},{6,7},{7,8},{8,9},{9,10},{10,1... | collective-permute-start | bytes 1966088 | tf_op jit(solution)/vmap(transpose(jvp()))/dot_general | solution.py:21
  1867.9 862.4 %all-gather.12.cloned.1.call-start = ((), (), s32[]{:S(2)}) async-start(), calls=%async_computation.1 | async-start | bytes 21626880 | tf_op jit(solution)/reshape | solution.py:52
  1890.3 31.7 %collective-permute-start.2 = (f32[5120,32]{0,1:T(8,128)}, f32[5120,32]{0,1:T(8,128)S(1)}, u32[]{:S(2)}, u32[]{:S(2)}) collective-permute-start(f32[5120,32]{0,1:T(8,128)} %get-tuple-element.456), channel_id=5, source_target_pairs={{0,1},{1,2},{2,3},{3,4},{4,5},{5,6},{6,7},{7,8},{8,9},{9,10},{10,1... | collective-permute-start | bytes 1966088 | tf_op jit(solution)/vmap(transpose(jvp()))/dot_general | solution.py:20
  1890.3 32.6 %collective-permute-start.3 = (f32[5120,32]{0,1:T(8,128)S(1)}, f32[5120,32]{0,1:T(8,128)}, u32[]{:S(2)}, u32[]{:S(2)}) collective-permute-start(f32[5120,32]{0,1:T(8,128)S(1)} %get-tuple-element.457), channel_id=4, source_target_pairs={{0,31},{1,0},{2,1},{3,2},{4,3},{5,4},{6,5},{7,6},{8,7},{9,8},{10,9... | collective-permute-start | bytes 1966088 | tf_op jit(solution)/vmap(transpose(jvp()))/dot_general | solution.py:20
  1926.3 32.5 %collective-permute-start = (f32[5120,32]{0,1:T(8,128)S(1)}, f32[5120,32]{0,1:T(8,128)}, u32[]{:S(2)}, u32[]{:S(2)}) collective-permute-start(f32[5120,32]{0,1:T(8,128)S(1)} %broadcast_select_fusion.24), channel_id=3, source_target_pairs={{0,1},{1,2},{2,3},{3,4},{4,5},{5,6},{6,7},{7,8},{8,9},{9,10},{10,1... | collective-permute-start | bytes 1966088 | tf_op jit(solution)/vmap(transpose(jvp()))/dot_general | solution.py:20
  1927.3 31.6 %collective-permute-start.1 = (f32[5120,32]{0,1:T(8,128)}, f32[5120,32]{0,1:T(8,128)S(1)}, u32[]{:S(2)}, u32[]{:S(2)}) collective-permute-start(f32[5120,32]{0,1:T(8,128)} %broadcast_select_fusion.25), channel_id=2, source_target_pairs={{0,31},{1,0},{2,1},{3,2},{4,3},{5,4},{6,5},{7,6},{8,7},{9,8},{10,9... | collective-permute-start | bytes 1966088 | tf_op jit(solution)/vmap(transpose(jvp()))/dot_general | solution.py:20
  1960.9 24.8 collective-permute-start.2
  1960.9 25.6 collective-permute-start.3
  1990.0 33.2 %collective-permute-start = (f32[5120,32]{0,1:T(8,128)S(1)}, f32[5120,32]{0,1:T(8,128)}, u32[]{:S(2)}, u32[]{:S(2)}) collective-permute-start(f32[5120,32]{0,1:T(8,128)S(1)} %broadcast_select_fusion.24), channel_id=3, source_target_pairs={{0,1},{1,2},{2,3},{3,4},{4,5},{5,6},{6,7},{7,8},{8,9},{9,10},{10,1... | collective-permute-start | bytes 1966088 | tf_op jit(solution)/vmap(transpose(jvp()))/dot_general | solution.py:20
  1991.0 32.3 %collective-permute-start.1 = (f32[5120,32]{0,1:T(8,128)}, f32[5120,32]{0,1:T(8,128)S(1)}, u32[]{:S(2)}, u32[]{:S(2)}) collective-permute-start(f32[5120,32]{0,1:T(8,128)} %broadcast_select_fusion.25), channel_id=2, source_target_pairs={{0,31},{1,0},{2,1},{3,2},{4,3},{5,4},{6,5},{7,6},{8,7},{9,8},{10,9... | collective-permute-start | bytes 1966088 | tf_op jit(solution)/vmap(transpose(jvp()))/dot_general | solution.py:20
  2025.3 33.0 %collective-permute-start.2 = (f32[5120,32]{0,1:T(8,128)}, f32[5120,32]{0,1:T(8,128)S(1)}, u32[]{:S(2)}, u32[]{:S(2)}) collective-permute-start(f32[5120,32]{0,1:T(8,128)} %get-tuple-element.456), channel_id=5, source_target_pairs={{0,1},{1,2},{2,3},{3,4},{4,5},{5,6},{6,7},{7,8},{8,9},{9,10},{10,1... | collective-permute-start | bytes 1966088 | tf_op jit(solution)/vmap(transpose(jvp()))/dot_general | solution.py:20
  2032.2 28.9 collective-permute-start.3
  2193.1 20.5 collective-permute-start
  2278.4 433.9 %collective-permute-start.24 = (f32[5120,32]{0,1:T(8,128)}, f32[5120,32]{0,1:T(8,128)}, u32[]{:S(2)}, u32[]{:S(2)}) collective-permute-start(f32[5120,32]{0,1:T(8,128)} %get-tuple-element.37), channel_id=6, source_target_pairs={{0,1},{1,2},{2,3},{3,4},{4,5},{5,6},{6,7},{7,8},{8,9},{9,10},{10,1... | collective-permute-start | bytes 1966088 | tf_op jit(solution)/vmap(transpose(jvp()))/dot_general | solution.py:20
  2285.2 574.6 %all-gather.10.cloned.1.call-start = ((), (), s32[]{:S(2)}) async-start(), calls=%async_computation | async-start | bytes 21626880 | tf_op jit(solution)/reshape | solution.py:52
  2306.9 32.2 %collective-permute-start.6 = (f32[5120,32]{0,1:T(8,128)}, f32[5120,32]{0,1:T(8,128)S(1)}, u32[]{:S(2)}, u32[]{:S(2)}) collective-permute-start(f32[5120,32]{0,1:T(8,128)} %get-tuple-element.465), channel_id=11, source_target_pairs={{0,1},{1,2},{2,3},{3,4},{4,5},{5,6},{6,7},{7,8},{8,9},{9,10},{10,1... | collective-permute-start | bytes 1966088 | tf_op jit(solution)/vmap(transpose(jvp()))/dot_general | solution.py:20
  2306.9 33.0 %collective-permute-start.7 = (f32[5120,32]{0,1:T(8,128)S(1)}, f32[5120,32]{0,1:T(8,128)}, u32[]{:S(2)}, u32[]{:S(2)}) collective-permute-start(f32[5120,32]{0,1:T(8,128)S(1)} %get-tuple-element.466), channel_id=10, source_target_pairs={{0,31},{1,0},{2,1},{3,2},{4,3},{5,4},{6,5},{7,6},{8,7},{9,8},{10,9... | collective-permute-start | bytes 1966088 | tf_op jit(solution)/vmap(transpose(jvp()))/dot_general | solution.py:20
  2343.4 32.6 %collective-permute-start.4 = (f32[5120,32]{0,1:T(8,128)S(1)}, f32[5120,32]{0,1:T(8,128)}, u32[]{:S(2)}, u32[]{:S(2)}) collective-permute-start(f32[5120,32]{0,1:T(8,128)S(1)} %broadcast_select_fusion.26), channel_id=9, source_target_pairs={{0,1},{1,2},{2,3},{3,4},{4,5},{5,6},{6,7},{7,8},{8,9},{9,10},{10,1... | collective-permute-start | bytes 1966088 | tf_op jit(solution)/vmap(transpose(jvp()))/dot_general | solution.py:20
  2344.4 31.9 %collective-permute-start.5 = (f32[5120,32]{0,1:T(8,128)}, f32[5120,32]{0,1:T(8,128)S(1)}, u32[]{:S(2)}, u32[]{:S(2)}) collective-permute-start(f32[5120,32]{0,1:T(8,128)} %broadcast_select_fusion.27), channel_id=8, source_target_pairs={{0,31},{1,0},{2,1},{3,2},{4,3},{5,4},{6,5},{7,6},{8,7},{9,8},{10,9... | collective-permute-start | bytes 1966088 | tf_op jit(solution)/vmap(transpose(jvp()))/dot_general | solution.py:20
  2378.4 26.3 collective-permute-start.6
  2381.6 24.0 collective-permute-start.7
  2409.0 34.5 %collective-permute-start.4 = (f32[5120,32]{0,1:T(8,128)S(1)}, f32[5120,32]{0,1:T(8,128)}, u32[]{:S(2)}, u32[]{:S(2)}) collective-permute-start(f32[5120,32]{0,1:T(8,128)S(1)} %broadcast_select_fusion.26), channel_id=9, source_target_pairs={{0,1},{1,2},{2,3},{3,4},{4,5},{5,6},{6,7},{7,8},{8,9},{9,10},{10,1... | collective-permute-start | bytes 1966088 | tf_op jit(solution)/vmap(transpose(jvp()))/dot_general | solution.py:20
  2409.9 33.5 %collective-permute-start.5 = (f32[5120,32]{0,1:T(8,128)}, f32[5120,32]{0,1:T(8,128)S(1)}, u32[]{:S(2)}, u32[]{:S(2)}) collective-permute-start(f32[5120,32]{0,1:T(8,128)} %broadcast_select_fusion.27), channel_id=8, source_target_pairs={{0,31},{1,0},{2,1},{3,2},{4,3},{5,4},{6,5},{7,6},{8,7},{9,8},{10,9... | collective-permute-start | bytes 1966088 | tf_op jit(solution)/vmap(transpose(jvp()))/dot_general | solution.py:20
  2445.6 33.4 %collective-permute-start.6 = (f32[5120,32]{0,1:T(8,128)}, f32[5120,32]{0,1:T(8,128)S(1)}, u32[]{:S(2)}, u32[]{:S(2)}) collective-permute-start(f32[5120,32]{0,1:T(8,128)} %get-tuple-element.465), channel_id=11, source_target_pairs={{0,1},{1,2},{2,3},{3,4},{4,5},{5,6},{6,7},{7,8},{8,9},{9,10},{10,1... | collective-permute-start | bytes 1966088 | tf_op jit(solution)/vmap(transpose(jvp()))/dot_general | solution.py:20
  2516.1 20.8 collective-permute-start.7
  (248 other events, 5422.3 us)
Sparse Core Ops, SparseCore 0:
  1868.0 194.7 all-gather.13
  2285.4 193.1 all-gather.11
  2730.4 129.3 all-gather.9
where the time goes:
time: 2920 us; the launch traced here: 2910 us
  waiting for transfers between devices  1010 us (35%)
  matrix products  903 us (31%)
  starting transfers between devices  548 us (19%)
  other arithmetic  285 us (10%)
  local copies, waits for them, and re-layouts  146 us (5%)
    dot_general x66, waiting for transfers between devices, matmul(): jnp.dot(a, w, preferred_element_type=jnp.float32).astype(jnp.bfloat16)  341 us
    dot_general x35, matrix products, layer(): up = jnp.dot(a, w['w_up'], preferred_element_type=jnp.float32)  337 us
    dot_general x66, waiting for transfers between devices, layer(): gate = jnp.dot(a, w['w_gate'], preferred_element_type=jnp.float32)  323 us
    dot_general x35, matrix products, layer(): gate = jnp.dot(a, w['w_gate'], preferred_element_type=jnp.float32)  293 us
    dot_general x35, matrix products, matmul(): jnp.dot(a, w, preferred_element_type=jnp.float32).astype(jnp.bfloat16)  273 us
    dot_general x66, waiting for transfers between devices, layer(): up = jnp.dot(a, w['w_up'], preferred_element_type=jnp.float32)  216 us
    dot_general x66, starting transfers between devices, layer(): gate = jnp.dot(a, w['w_gate'], preferred_element_type=jnp.float32)  200 us
    dot_general x66, starting transfers between devices, matmul(): jnp.dot(a, w, preferred_element_type=jnp.float32).astype(jnp.bfloat16)  175 us
  transfers between devices with their start and end apart: 201, of which 114 were waited for; matrix products, arithmetic and copies ran while one was open for 35% of the time, Pallas kernels for 0%

commit v1 on v0

v1 whole, which is shorter than its diff:
```python
import jax
import jax.numpy as jnp
from jax import lax
from jax.sharding import PartitionSpec as P

NAMES = ("w_gate", "w_up", "w_down")


def matmul(a, w):
    return jnp.dot(a, w, preferred_element_type=jnp.float32).astype(jnp.bfloat16)


def normed(h):
    wide = h.astype(jnp.float32)
    scale = lax.rsqrt(jnp.mean(wide**2, -1, keepdims=True) + 1e-6)
    return (wide * scale).astype(jnp.bfloat16)


def layer(h, w):
    a = normed(h)
    gate = jnp.dot(a, w["w_gate"], preferred_element_type=jnp.float32)
    up = jnp.dot(a, w["w_up"], preferred_element_type=jnp.float32)
    return h + matmul((jax.nn.silu(gate) * up).astype(jnp.bfloat16), w["w_down"])


def adamw(w, m, v, g):
    m = 0.9 * m + 0.1 * g
    v = 0.95 * v + 0.05 * g * g
    step = m * lax.rsqrt(v + 1e-8) + 0.1 * w
    return (w - 0.02 * step).astype(jnp.bfloat16), m, v


def solution(mesh):
    def step(x, dy, *arrays):
        weights, m, v = (arrays[i : i + 3] for i in (0, 3, 6))
        x, dy = x[0], dy[0]
        layers = weights[0].shape[0]
        per_layer = [{name: w[number] for name, w in zip(NAMES, weights, strict=True)} for number in range(layers)]

        def stack(per_layer):
            h = x
            for w in per_layer:
                h = layer(h, w)
            return h

        _, back = jax.vjp(stack, per_layer)
        grads = back(dy)[0]
        me = lax.axis_index("dp")
        new = {name: [None] * layers for name in NAMES}
        for number in reversed(range(layers)):
            for i, name in reversed(list(enumerate(NAMES))):
                g = lax.psum_scatter(grads[number][name], "dp", scatter_dimension=0, tiled=True)
                rows = g.shape[0]
                w = lax.dynamic_slice_in_dim(weights[i][number], me * rows, rows, 0)
                w, nm, nv = adamw(w.astype(jnp.float32), m[i][number], v[i][number], g.astype(jnp.float32))
                new[name][number] = (lax.all_gather(w, "dp", axis=0, tiled=True), nm, nv)
        return tuple(jnp.stack([new[name][number][which] for number in range(layers)]) for which in range(3) for name in NAMES)

    whole, rows, seq = P(None, None, None), P(None, "dp", None), P(("rep", "dp"), None, None)
    return jax.shard_map(
        step,
        mesh=mesh,
        in_specs=(seq, seq) + (whole,) * 3 + (rows,) * 6,
        out_specs=(P("rep", None, None),) * 3 + (P("rep", "dp", None),) * 6,
        check_vma=False,
    )
```

time: 2920 us -> 1800 us (0.62)
  starting transfers between devices: 548 us -> 0.49 us
  matrix products: 903 us -> 533 us
  other arithmetic: 285 us -> 78.2 us
  waiting for transfers between devices: 1010 us -> 1100 us
  local copies, waits for them, and re-layouts: 146 us -> 64.1 us
    dot_general x198 -> x0, waiting for transfers between devices: 880 us -> none  [the longest x66 341 us: matmul(): jnp.dot(a, w, preferred_element_type=jnp.float32).astype(jnp.bfloat16)]
    reduce_scatter x0 -> x6, waiting for transfers between devices: none -> 615 us  [step(): lax.psum_scatter(grads[number][name], 'dp', scatter_dimension=0, tiled=True)]
    dot_general x198 -> x0, starting transfers between devices: 548 us -> none  [the longest x66 200 us: layer(): gate = jnp.dot(a, w['w_gate'], preferred_element_type=jnp.float32)]
    all_gather x0 -> x6, waiting for transfers between devices: none -> 480 us  [step(): new[name][number] = (lax.all_gather(w, 'dp', axis=0, tiled=True), nm, nv)]
    dot_general x192 -> x0, other arithmetic: 251 us -> none  [the longest x32 77.4 us: layer(): up = jnp.dot(a, w['w_up'], preferred_element_type=jnp.float32)]
    dot_general x35 -> x5, matrix products: 337 us -> 190 us  [layer(): up = jnp.dot(a, w['w_up'], preferred_element_type=jnp.float32)]
    reshape x3 -> x0, waiting for transfers between devices: 130 us -> none  [step(): t.reshape(-1, *t.shape[2:])]
    dot_general x35 -> x5, matrix products: 273 us -> 154 us  [matmul(): jnp.dot(a, w, preferred_element_type=jnp.float32).astype(jnp.bfloat16)]
  transfers between devices with their start and end apart: 201 -> 12, of which waited for: 114 -> 11; matrix products, arithmetic and copies ran while one was open for 35% -> 21% of each run, Pallas kernels for 0% -> 0%
where the time goes in v1:
time: 1800 us; the launch traced here: 1790 us
  waiting for transfers between devices  1100 us (61%)
  matrix products  533 us (30%)
  other arithmetic  78.2 us (4%)
  local copies, waits for them, and re-layouts  64.1 us (4%)
    reduce_scatter x6, waiting for transfers between devices, step(): lax.psum_scatter(grads[number][name], 'dp', scatter_dimension=0, tiled=True)  615 us
    all_gather x6, waiting for transfers between devices, step(): new[name][number] = (lax.all_gather(w, 'dp', axis=0, tiled=True), nm, nv)  480 us
    dot_general x5, matrix products, layer(): gate = jnp.dot(a, w['w_gate'], preferred_element_type=jnp.float32)  190 us
    dot_general x5, matrix products, layer(): up = jnp.dot(a, w['w_up'], preferred_element_type=jnp.float32)  190 us
    dot_general x5, matrix products, matmul(): jnp.dot(a, w, preferred_element_type=jnp.float32).astype(jnp.bfloat16)  154 us
    another operation x6, other arithmetic, step(): jnp.stack([new[name][number][which] for number in range(layers)])  58.1 us
  transfers between devices with their start and end apart: 12, of which 11 were waited for; matrix products, arithmetic and copies ran while one was open for 21% of the time, Pallas kernels for 0%

profile of v1, /device:TPU:0, one launch (start us, length us, event | category | flops | bytes accessed | tf_op | source)
XLA Modules:
  0.0 1787.7 jit_solution(6912772060067667709)
XLA Ops:
  7.2 0.0 reduce-scatter.17.cloned.1.call-start
  7.2 6.5 copy.20
  13.8 3.1 fusion.36
  16.8 29.8 %fusion.28 = f32[2048,5120]{1,0:T(8,128)} fusion(bf16[1,2048,1024]{2,1,0:T(8,128)(2,1)} %param.11, f32[2048]{0:T(1024)S(1)} %add_rsqrt_fusion, bf16[2,1024,5120]{2,1,0:T(8,128)(2,1)} %param.13), kind=kOutput, calls=%fused_computation.49 | convolution fusion | flops 21481127936 | bytes 56631296 | tf_op jit(solution)/shard_map/jvp()/dot_general | solution.py:21
  46.6 49.5 %multiply_convert_fusion.1 = (bf16[2048,5120]{1,0:T(8,128)(2,1)}, f32[2048,5120]{1,0:T(8,128)}) fusion(f32[2048,5120]{1,0:T(8,128)} %fusion.28, bf16[2,1024,5120]{2,1,0:T(8,128)(2,1)} %param.14, bf16[1,2048,1024]{2,1,0:T(8,128)(2,1)} %param.11, f32[2048]{0:T(1024)S(1)} %add_rsqrt_fusion), kind=kOutput, calls=%fused_computation.17 | convolution fusion | flops 21544042496 | bytes 119545856 | tf_op jit(solution)/shard_map/jvp()/dot_general | solution.py:22
  96.1 30.1 %fusion.40 = (f32[2048]{0:T(1024)S(1)}, bf16[2048,1024]{0,1:T(8,128)(2,1)}) fusion(bf16[2048,5120]{1,0:T(8,128)(2,1)} %get-tuple-element.33, bf16[2,5120,1024]{2,1,0:T(8,128)(2,1)} %param.15, bf16[1,2048,1024]{1,2,0:T(8,128)(2,1)} %copy.20), kind=kOutput, calls=%fused_computation.61 | convolution fusion | flops 21485320192 | bytes 39854080 | tf_op jit(solution)/shard_map/jvp()/dot_general | solution.py:10
  126.2 29.8 %convolution_convert_fusion.1 = bf16[2048,5120]{1,0:T(8,128)(2,1)} fusion(bf16[1,2048,1024]{2,1,0:T(8,128)(2,1)} %param.12, bf16[2,5120,1024]{2,1,0:T(8,128)(2,1)} %param.15), kind=kOutput, calls=%fused_computation.28 | convolution fusion | flops 21485322240 | bytes 35651584 | tf_op jit(solution)/shard_map/transpose(jvp())/dot_general | solution.py:10
  156.0 42.4 %fusion.15 = f32[2048,5120]{1,0:T(8,128)} fusion(bf16[2048,1024]{0,1:T(8,128)(2,1)} %get-tuple-element.36, f32[2048]{0:T(1024)S(1)} %fusion.102, bf16[2,1024,5120]{2,1,0:T(8,128)(2,1)} %param.14), kind=kOutput, calls=%fused_computation.36 | convolution fusion | flops 21481127936 | bytes 56631296 | tf_op jit(solution)/shard_map/jvp()/dot_general | solution.py:22
  198.5 57.3 %fusion.2 = (bf16[2048,5120]{1,0:T(8,128)(2,1)}, f32[2048,5120]{1,0:T(8,128)}) fusion(f32[2048,5120]{1,0:T(8,128)} %fusion.15, bf16[2048,5120]{1,0:T(8,128)(2,1)} %convolution_convert_fusion.1, bf16[2,1024,5120]{2,1,0:T(8,128)(2,1)} %param.13, bf16[2048,1024]{0,1:T(8,128)(2,1)} %get-tuple-element.36, f32[2048]{0:T(1024)S(1)} %fusion.102), kind=kOutput, calls=%fused_computation.8 | convolution fusion | flops 21606957056 | bytes 140517376 | tf_op jit(solution)/shard_map/jvp()/dot_general | solution.py:21
  255.8 37.1 %fusion.30 = bf16[5120,1024]{1,0:T(8,128)(2,1)} fusion(f32[2048,5120]{1,0:T(8,128)} %fusion.15, bf16[1,2048,1024]{2,1,0:T(8,128)(2,1)} %param.12, f32[2048,5120]{1,0:T(8,128)} %get-tuple-element.38), kind=kOutput, calls=%fused_computation.51 | convolution fusion | flops 21542993920 | bytes 98566144 | tf_op jit(solution)/shard_map/transpose(jvp())/dot_general | solution.py:10
  292.9 0.0 reduce-scatter.17.cloned.1.call-update
  292.9 0.0 reduce-scatter.15.cloned.1.call-start
  292.9 7.0 copy.21
  299.9 32.4 %fusion.12 = bf16[2048,1024]{0,1:T(8,128)(2,1)} fusion(bf16[2048,5120]{1,0:T(8,128)(2,1)} %convolution_convert_fusion.1, bf16[2,1024,5120]{2,1,0:T(8,128)(2,1)} %param.14, f32[2048,5120]{1,0:T(8,128)} %get-tuple-element.38), kind=kOutput, calls=%fused_computation.21 | convolution fusion | flops 21537751040 | bytes 77594624 | tf_op jit(solution)/shard_map/transpose(jvp())/dot_general | solution.py:22
  332.3 30.7 %fusion.42 = (f32[2048]{0:T(1024)S(1)}, bf16[2048,1024]{0,1:T(8,128)(2,1)}) fusion(bf16[2048,1024]{0,1:T(8,128)(2,1)} %get-tuple-element.36, bf16[2048,1024]{0,1:T(8,128)(2,1)} %fusion.12, bf16[2048,5120]{1,0:T(8,128)(2,1)} %get-tuple-element.37, bf16[2,1024,5120]{2,1,0:T(8,128)(2,1)} %param.13), kind=kOutput, calls=%fused_computation.63 | convolution fusion | flops 21485320192 | bytes 44048384 | tf_op jit(solution)/shard_map/transpose(jvp())/dot_general | solution.py:21
  363.0 5.3 fusion.45
  368.4 1.9 copy-done.1
  370.3 27.0 %convolution_convert_fusion.2 = bf16[5120,1024]{1,0:T(8,128)(2,1)} fusion(bf16[2048,5120]{1,0:T(8,128)(2,1)} %get-tuple-element.33, bf16[2048,1024]{0,1:T(8,128)(2,1)S(1)} %fusion.45), kind=kOutput, calls=%fused_computation.55 | convolution fusion | flops 21480079360 | bytes 35651584 | tf_op jit(solution)/shard_map/transpose(jvp())/dot_general | solution.py:10
  397.3 0.0 reduce-scatter.15.cloned.1.call-update
  397.3 0.0 reduce-scatter.13.cloned.1.call-start
  397.4 32.5 %fusion.31 = bf16[1024,5120]{1,0:T(8,128)(2,1)} fusion(bf16[2048,5120]{1,0:T(8,128)(2,1)} %convolution_convert_fusion.1, bf16[2048,1024]{0,1:T(8,128)(2,1)} %get-tuple-element.36, f32[2048]{0:T(1024)S(1)} %copy-done.7, f32[2048,5120]{1,0:T(8,128)} %get-tuple-element.38), kind=kOutput, calls=%fused_computation.52 | convolution fusion | flops 21549285376 | bytes 77602816 | tf_op jit(solution)/shard_map/transpose(jvp())/dot_general | solution.py:22
  429.9 0.0 reduce-scatter.13.cloned.1.call-update
  429.9 0.0 reduce-scatter.11.cloned.1.call-start
  430.0 29.6 %convolution_convert_fusion = bf16[2048,5120]{1,0:T(8,128)(2,1)} fusion(bf16[2048,1024]{0,1:T(8,128)(2,1)} %copy-done.1, bf16[2,5120,1024]{2,1,0:T(8,128)(2,1)} %param.15), kind=kOutput, calls=%fused_computation.27 | convolution fusion | flops 21485322240 | bytes 35651584 | tf_op jit(solution)/shard_map/transpose(jvp())/dot_general | solution.py:10
  459.5 32.7 %fusion.35 = bf16[1024,5120]{1,0:T(8,128)(2,1)} fusion(bf16[2048,5120]{1,0:T(8,128)(2,1)} %convolution_convert_fusion, f32[2048,5120]{1,0:T(8,128)} %fusion.28, bf16[1,2048,1024]{1,2,0:T(8,128)(2,1)} %copy.20, f32[2048]{0:T(1024)S(1)} %copy-done.11), kind=kOutput, calls=%fused_computation.54 | convolution fusion | flops 21549285376 | bytes 77602816 | tf_op jit(solution)/shard_map/transpose(jvp())/dot_general | solution.py:22
  492.2 0.0 reduce-scatter.9.cloned.1.call-start
  492.3 28.2 %convolution_convert_fusion.3 = bf16[1024,5120]{1,0:T(8,128)(2,1)} fusion(bf16[2048,5120]{1,0:T(8,128)(2,1)} %get-tuple-element.37, bf16[2048,1024]{0,1:T(8,128)(2,1)} %get-tuple-element.36, f32[2048]{0:T(1024)S(1)} %copy-done.7), kind=kOutput, calls=%fused_computation.56 | convolution fusion | flops 21481127936 | bytes 35659776 | tf_op jit(solution)/shard_map/transpose(jvp())/dot_general | solution.py:21
  520.5 0.0 reduce-scatter.9.cloned.1.call-update
  520.5 0.0 reduce-scatter.7.cloned.1.call-start
  520.5 44.2 %fusion.32 = bf16[1024,5120]{1,0:T(8,128)(2,1)} fusion(f32[2048,5120]{1,0:T(8,128)} %fusion.28, f32[2048,5120]{1,0:T(8,128)} %get-tuple-element.34, bf16[2048,5120]{1,0:T(8,128)(2,1)} %convolution_convert_fusion, bf16[1,2048,1024]{1,2,0:T(8,128)(2,1)} %copy.20, f32[2048]{0:T(1024)S(1)} %copy-done.11), kind=kOutput, calls=%fused_computation.53 | convolution fusion | flops 21601714176 | bytes 119545856 | tf_op jit(solution)/shard_map/transpose(jvp())/dot_general | solution.py:21
  564.7 0.0 all-gather.15.cloned.1.call-start
  564.8 16.1 fusion.117
  580.9 28.4 %reduce-scatter.15.cloned.1.call-done = bf16[160,1024]{1,0:T(8,128)(2,1)} async-done(((bf16[5120,1024]{1,0:T(8,128)(2,1)}), bf16[160,1024]{1,0:T(8,128)(2,1)}) %reduce-scatter.15.cloned.1.call-update) | async-done | bytes 327696 | tf_op jit(solution)/shard_map/reduce_scatter | solution.py:52
  609.2 3.7 fusion.80
  612.9 0.0 all-gather.17.cloned.1.call-start
  613.0 0.7 all-gather.17.cloned.1.call-update
  613.7 0.0 all-gather.11.cloned.1.call-start
  613.7 16.2 fusion.118
  629.9 136.5 %reduce-scatter.13.cloned.1.call-done = bf16[32,5120]{1,0:T(8,128)(2,1)} async-done(((bf16[1024,5120]{1,0:T(8,128)(2,1)}), bf16[32,5120]{1,0:T(8,128)(2,1)}) %reduce-scatter.13.cloned.1.call-update) | async-done | bytes 327696 | tf_op jit(solution)/shard_map/reduce_scatter | solution.py:52
  766.4 157.0 %reduce-scatter.11.cloned.1.call-done = bf16[32,5120]{1,0:T(8,128)(2,1)} async-done(((bf16[1024,5120]{1,0:T(8,128)(2,1)}), bf16[32,5120]{1,0:T(8,128)(2,1)}) %reduce-scatter.11.cloned.1.call-update) | async-done | bytes 327696 | tf_op jit(solution)/shard_map/reduce_scatter | solution.py:52
  923.4 3.9 fusion.74
  927.3 0.0 all-gather.11.cloned.1.call-update
  927.4 0.0 all-gather.13.cloned.1.call-start
  927.4 0.5 all-gather.13.cloned.1.call-update
  928.0 0.0 all-gather.7.cloned.1.call-start
  928.0 16.4 fusion.119
  944.4 136.0 %reduce-scatter.9.cloned.1.call-done = bf16[32,5120]{1,0:T(8,128)(2,1)} async-done(((bf16[1024,5120]{1,0:T(8,128)(2,1)}), bf16[32,5120]{1,0:T(8,128)(2,1)}) %reduce-scatter.9.cloned.1.call-update) | async-done | bytes 327696 | tf_op jit(solution)/shard_map/reduce_scatter | solution.py:52
  1080.4 157.6 %reduce-scatter.7.cloned.1.call-done = bf16[32,5120]{1,0:T(8,128)(2,1)} async-done(((bf16[1024,5120]{1,0:T(8,128)(2,1)}), bf16[32,5120]{1,0:T(8,128)(2,1)}) %reduce-scatter.7.cloned.1.call-update) | async-done | bytes 327696 | tf_op jit(solution)/shard_map/reduce_scatter | solution.py:52
  1238.0 4.1 fusion.68
  1242.1 0.0 all-gather.7.cloned.1.call-update
  1242.1 0.0 all-gather.9.cloned.1.call-start
  1242.1 0.5 all-gather.9.cloned.1.call-update
  1242.7 1.7 pad_maximum_fusion.5
  1244.4 3.2 pad_maximum_fusion.4
  1247.6 1.7 pad_maximum_fusion.3
  1249.3 75.6 %all-gather.15.cloned.1.call-done = bf16[5120,1024]{1,0:T(8,128)(2,1)} async-done(((bf16[160,1024]{1,0:T(8,128)(2,1)}), bf16[5120,1024]{1,0:T(8,128)(2,1)}) %all-gather.15.cloned.1.call-update) | async-done | bytes 10485776 | tf_op jit(solution)/shard_map/all_gather | solution.py:56
  1324.9 87.7 %all-gather.17.cloned.1.call-done = bf16[5120,1024]{1,0:T(8,128)(2,1)} async-done(((bf16[160,1024]{1,0:T(8,128)(2,1)}), bf16[5120,1024]{1,0:T(8,128)(2,1)}) %all-gather.17.cloned.1.call-update) | async-done | bytes 10485776 | tf_op jit(solution)/shard_map/all_gather | solution.py:56
  1412.6 17.2 pad_maximum_fusion.2
  1429.8 70.7 %all-gather.11.cloned.1.call-done = bf16[1024,5120]{1,0:T(8,128)(2,1)} async-done(((bf16[32,5120]{1,0:T(8,128)(2,1)}), bf16[1024,5120]{1,0:T(8,128)(2,1)}) %all-gather.11.cloned.1.call-update) | async-done | bytes 10485776 | tf_op jit(solution)/shard_map/all_gather | solution.py:56
  1500.5 87.6 %all-gather.13.cloned.1.call-done = bf16[1024,5120]{1,0:T(8,128)(2,1)} async-done(((bf16[32,5120]{1,0:T(8,128)(2,1)}), bf16[1024,5120]{1,0:T(8,128)(2,1)}) %all-gather.13.cloned.1.call-update) | async-done | bytes 10485776 | tf_op jit(solution)/shard_map/all_gather | solution.py:56
  1588.1 17.2 pad_maximum_fusion.1
  1605.3 70.6 %all-gather.7.cloned.1.call-done = bf16[1024,5120]{1,0:T(8,128)(2,1)} async-done(((bf16[32,5120]{1,0:T(8,128)(2,1)}), bf16[1024,5120]{1,0:T(8,128)(2,1)}) %all-gather.7.cloned.1.call-update) | async-done | bytes 10485776 | tf_op jit(solution)/shard_map/all_gather | solution.py:56
  1675.9 87.7 %all-gather.9.cloned.1.call-done = bf16[1024,5120]{1,0:T(8,128)(2,1)} async-done(((bf16[32,5120]{1,0:T(8,128)(2,1)}), bf16[1024,5120]{1,0:T(8,128)(2,1)}) %all-gather.9.cloned.1.call-update) | async-done | bytes 10485776 | tf_op jit(solution)/shard_map/all_gather | solution.py:56
  1763.5 17.2 pad_maximum_fusion
  (30 shorter events, 0.1 us)
Async XLA Ops:
  7.2 573.7 %reduce-scatter.17.cloned.1.call-start = ((), (), s32[]{:S(2)}) async-start(), calls=%async_computation.16 | async-start | bytes 10813440 | tf_op jit(solution)/shard_map/reduce_scatter | solution.py:52
  16.8 29.8 %copy-start.10 = (f32[2048]{0:T(1024)}, f32[2048]{0:T(1024)S(1)}, u32[]{:S(2)}) copy-start(f32[2048]{0:T(1024)S(1)} %add_rsqrt_fusion) | copy-start | bytes 24580
  126.2 29.8 %copy-start.8 = (f32[2048]{0:T(1024)}, f32[2048]{0:T(1024)S(1)}, u32[]{:S(2)}) copy-start(f32[2048]{0:T(1024)S(1)} %get-tuple-element.35) | copy-start | bytes 24580
  126.2 72.3 %copy-start.6 = (f32[2048]{0:T(1024)}, f32[2048]{0:T(1024)S(1)}, u32[]{:S(2)}) copy-start(f32[2048]{0:T(1024)S(1)} %fusion.102) | copy-start | bytes 24580
  292.9 316.4 %reduce-scatter.15.cloned.1.call-start = ((), (), s32[]{:S(2)}) async-start(), calls=%async_computation.14 | async-start | bytes 10813440 | tf_op jit(solution)/shard_map/reduce_scatter | solution.py:52
  332.3 30.7 %copy-start.9 = (f32[2048]{0:T(1024)S(1)}, f32[2048]{0:T(1024)}, u32[]{:S(2)}) copy-start(f32[2048]{0:T(1024)} %copy-done.8) | copy-start | bytes 24580
  332.3 30.7 %copy-start = (bf16[1,2048,1024]{1,2,0:T(8,128)(2,1)S(1)}, bf16[1,2048,1024]{1,2,0:T(8,128)(2,1)}, u32[]{:S(2)}) copy-start(bf16[1,2048,1024]{1,2,0:T(8,128)(2,1)} %copy.21) | copy-start | bytes 12582916
  332.3 30.7 %copy-start.7 = (f32[2048]{0:T(1024)S(1)}, f32[2048]{0:T(1024)}, u32[]{:S(2)}) copy-start(f32[2048]{0:T(1024)} %copy-done.6) | copy-start | bytes 24580
  368.4 1.9 copy-start.1
  397.3 369.0 %reduce-scatter.13.cloned.1.call-start = ((), (), s32[]{:S(2)}) async-start(), calls=%async_computation.12 | async-start | bytes 10813440 | tf_op jit(solution)/shard_map/reduce_scatter | solution.py:52
  429.9 29.6 %copy-start.11 = (f32[2048]{0:T(1024)S(1)}, f32[2048]{0:T(1024)}, u32[]{:S(2)}) copy-start(f32[2048]{0:T(1024)} %copy-done.10) | copy-start | bytes 24580
  429.9 493.5 %reduce-scatter.11.cloned.1.call-start = ((), (), s32[]{:S(2)}) async-start(), calls=%async_computation.10 | async-start | bytes 10813440 | tf_op jit(solution)/shard_map/reduce_scatter | solution.py:52
  492.2 588.2 %reduce-scatter.9.cloned.1.call-start = ((), (), s32[]{:S(2)}) async-start(), calls=%async_computation.8 | async-start | bytes 10813440 | tf_op jit(solution)/shard_map/reduce_scatter | solution.py:52
  520.5 717.5 %reduce-scatter.7.cloned.1.call-start = ((), (), s32[]{:S(2)}) async-start(), calls=%async_computation.6 | async-start | bytes 10813440 | tf_op jit(solution)/shard_map/reduce_scatter | solution.py:52
  564.7 760.2 %all-gather.15.cloned.1.call-start = ((), (), s32[]{:S(2)}) async-start(), calls=%async_computation.15 | async-start | bytes 10813440 | tf_op jit(solution)/shard_map/all_gather | solution.py:56
  612.9 799.7 %all-gather.17.cloned.1.call-start = ((), (), s32[]{:S(2)}) async-start(), calls=%async_computation.17 | async-start | bytes 10813440 | tf_op jit(solution)/shard_map/all_gather | solution.py:56
  613.7 886.8 %all-gather.11.cloned.1.call-start = ((), (), s32[]{:S(2)}) async-start(), calls=%async_computation.11 | async-start | bytes 10813440 | tf_op jit(solution)/shard_map/all_gather | solution.py:56
  927.4 660.7 %all-gather.13.cloned.1.call-start = ((), (), s32[]{:S(2)}) async-start(), calls=%async_computation.13 | async-start | bytes 10813440 | tf_op jit(solution)/shard_map/all_gather | solution.py:56
  928.0 747.9 %all-gather.7.cloned.1.call-start = ((), (), s32[]{:S(2)}) async-start(), calls=%async_computation.7 | async-start | bytes 10813440 | tf_op jit(solution)/shard_map/all_gather | solution.py:56
  1242.1 521.4 %all-gather.9.cloned.1.call-start = ((), (), s32[]{:S(2)}) async-start(), calls=%async_computation.9 | async-start | bytes 10813440 | tf_op jit(solution)/shard_map/all_gather | solution.py:56
  1242.7 4.9 copy-start.2
  1242.7 4.9 copy-start.3
  1242.7 4.9 copy-start.4
  1242.7 4.9 copy-start.5
Sparse Core Ops, SparseCore 0:
  293.0 159.1 reduce-scatter.16
  454.5 154.6 reduce-scatter.14
  611.6 154.7 reduce-scatter.12
  768.6 154.7 reduce-scatter.10
  925.5 154.7 reduce-scatter.8
  1083.1 154.7 reduce-scatter.6
  1240.8 84.0 all-gather.14
  1327.8 84.8 all-gather.16
  1415.5 84.8 all-gather.10
  1503.2 84.8 all-gather.12
  1591.0 84.8 all-gather.6
  1678.6 84.8 all-gather.8

commit v2 on v1

v2 whole, which is shorter than its diff:
```python
import functools
import jax, jax.numpy as jnp
from jax import lax
from jax.experimental import pallas as pl
from jax.experimental.pallas import tpu as pltpu
from jax.sharding import PartitionSpec as P

MESH = pl.DeviceIdType.MESH
f32, bf16 = jnp.float32, jnp.bfloat16

def idx(x, y, z, c):
    return ((x * 2 + y) * 4 + z) * 2 + c

class Me:
    def __init__(self):
        d = lax.axis_index("dp")
        self.c = lax.rem(d, 2)
        self.z = lax.rem(lax.div(d, 2), 4)
        self.y = lax.rem(lax.div(d, 8), 2)
        self.x = lax.div(d, 16)
    def core(self): return idx(self.x, self.y, self.z, 1 - self.c)
    def xn(self): return idx(1 - self.x, self.y, self.z, self.c)
    def yn(self): return idx(self.x, 1 - self.y, self.z, self.c)
    def zk(self, k): return idx(self.x, self.y, lax.rem(self.z + k, 4), self.c)

def barrier(me):
    sem = pltpu.get_barrier_semaphore()
    peers = [me.core(), me.xn(), me.yn()] + [me.zk(k) for k in (1, 2, 3)]
    for p in peers:
        pl.semaphore_signal(sem, inc=1, device_id={"dp": p}, device_id_type=MESH)
    pl.semaphore_wait(sem, len(peers))

def sel(k, a, b):
    return (1 - k) * a + k * b

class Sems:
    def __init__(self, send, recv):
        self.send, self.recv, self.n = send, recv, 0
    def copy(self, src, dst, dev):
        i = self.n; self.n += 1
        return pltpu.make_async_remote_copy(src_ref=src, dst_ref=dst, send_sem=self.send.at[i], recv_sem=self.recv.at[i],
                                            device_id={"dp": dev}, device_id_type=MESH)
SEMS_PER = 19

class Unit:
    def __init__(self, me, sems, layer, r, C, G, Wold, m, v, Wnew, mo, vo, bufs):
        self.me, self.sems, self.l, self.r, self.C = me, sems, layer, r, C
        self.G, self.Wold, self.m, self.v, self.W, self.mo, self.vo = G, Wold, m, v, Wnew, mo, vo
        self.R0, self.S0, self.R1, self.S1, self.R2, self.S2, self.R3 = bufs
        self.pending = []
        self.cp = {}
    def start(self, key, cps):
        self.cp[key] = cps
        for c in cps: c.start()
    def wait(self, key):
        for c in self.cp[key]: c.wait_recv()
    def drain(self):
        for cps in self.cp.values():
            for c in cps: c.wait_send()
    def s0(self):
        me, s = self.me, self.sems
        cps = []
        for x in range(2):
            for y in range(2):
                cps.append(s.copy(self.G.at[x, y, :, 1 - me.c], self.R0.at[x, y], me.core()))
        self.start("core", cps)
    def s1(self):
        me, h, C = self.me, self.r // 2, self.C
        x, y, z, c = me.x, me.y, me.z, me.c
        self.wait("core")
        def xyz(k, j): return sel(k, 1 - x, j // 4), sel(k, j // 4, 1 - y), j % 4
        def gm(k, j):
            a, b, d = xyz(k, j); return (a, b, d, c, k, 0)
        def rm(k, j):
            a, b, d = xyz(k, j); return (a, b, d, k, 0)
        def body(g, r0, o):
            o[...] = (g[...].astype(f32) + r0[...].astype(f32)).astype(bf16)
        N = None
        pltpu.emit_pipeline(body, grid=(2, 8),
            in_specs=[pl.BlockSpec((N, N, N, N, h, C), gm), pl.BlockSpec((N, N, N, h, C), rm)],
            out_specs=[pl.BlockSpec((N, N, h, C), lambda k, j: (k, j, 0, 0))])(self.G, self.R0, self.S0)
        self.start("xy1", [self.sems.copy(self.S0.at[0], self.R1.at[0], me.xn()), self.sems.copy(self.S0.at[1], self.R1.at[1], me.yn())])
    def s2(self):
        me, h, C = self.me, self.r // 2, self.C
        x, y, z, c = me.x, me.y, me.z, me.c
        self.wait("xy1")
        def gm(k, j): return (sel(k, x, 1 - x), sel(k, 1 - y, y), j, c, k, 0)
        def rm(k, j): return (sel(k, x, 1 - x), sel(k, 1 - y, y), j, k, 0)
        def r1(k, j): return (k, sel(k, 1 - y, 1 - x) * 4 + j, 0, 0)
        def body(g, r0, r1, o):
            o[...] = (g[...].astype(f32) + r0[...].astype(f32) + r1[...].astype(f32)).astype(bf16)
        N = None
        pltpu.emit_pipeline(body, grid=(2, 4),
            in_specs=[pl.BlockSpec((N, N, N, N, h, C), gm), pl.BlockSpec((N, N, N, h, C), rm), pl.BlockSpec((N, N, h, C), r1)],
            out_specs=[pl.BlockSpec((N, N, h, C), lambda k, j: (k, j, 0, 0))])(self.G, self.R0, self.R1, self.S1)
        self.start("xy2", [self.sems.copy(self.S1.at[0], self.R2.at[0], me.yn()), self.sems.copy(self.S1.at[1], self.R2.at[1], me.xn())])
    def s3(self):
        me, h, C = self.me, self.r // 2, self.C
        x, y, z, c = me.x, me.y, me.z, me.c
        self.wait("xy2")
        def zz(j): return lax.rem(z + 1 + j, 4)
        def gm(j, k): return (x, y, zz(j), c, k, 0)
        def rm(j, k): return (x, y, zz(j), k, 0)
        def r1(j, k): return (k, sel(k, y, x) * 4 + zz(j), 0, 0)
        def r2(j, k): return (k, zz(j), 0, 0)
        def body(g, r0, r1, r2, o):
            o[...] = (g[...].astype(f32) + r0[...].astype(f32) + r1[...].astype(f32) + r2[...].astype(f32)).astype(bf16)
        N = None
        pltpu.emit_pipeline(body, grid=(3, 2),
            in_specs=[pl.BlockSpec((N, N, N, N, h, C), gm), pl.BlockSpec((N, N, N, h, C), rm), pl.BlockSpec((N, N, h, C), r1), pl.BlockSpec((N, N, h, C), r2)],
            out_specs=[pl.BlockSpec((N, h, C), lambda j, k: (j, k, 0))])(self.G, self.R0, self.R1, self.R2, self.S2)
        self.start("z", [self.sems.copy(self.S2.at[k - 1], self.R3.at[k - 1], me.zk(k)) for k in (1, 2, 3)])
    def s4(self):
        me, h, C, l = self.me, self.r // 2, self.C, self.l
        x, y, z, c = me.x, me.y, me.z, me.c
        self.wait("z")
        N = None
        def body(g, r0, r1, r2, r3, w, m, v, wo, mo, vo):
            t = g[...].astype(f32) + r0[...].astype(f32) + r1[...].astype(f32) + r2[...].astype(f32)
            for k in range(3): t = t + r3[k].astype(f32)
            t = t.astype(bf16).astype(f32)
            mm = 0.9 * m[...] + 0.1 * t
            vv = 0.95 * v[...] + 0.05 * t * t
            ww = w[...].astype(f32)
            step = mm * lax.rsqrt(vv + 1e-8) + 0.1 * ww
            wo[...] = (ww - 0.02 * step).astype(bf16)
            mo[...] = mm
            vo[...] = vv
        wspec = pl.BlockSpec((N, N, N, N, N, h, C), lambda k: (l, x, y, z, c, k, 0))
        mspec = pl.BlockSpec((N, h, C), lambda k: (l, k, 0))
        pltpu.emit_pipeline(body, grid=(2,),
            in_specs=[pl.BlockSpec((N, N, N, N, h, C), lambda k: (x, y, z, c, k, 0)), pl.BlockSpec((N, N, N, h, C), lambda k: (x, y, z, k, 0)),
                      pl.BlockSpec((N, N, h, C), lambda k: (k, sel(k, y, x) * 4 + z, 0, 0)), pl.BlockSpec((N, N, h, C), lambda k: (k, z, 0, 0)),
                      pl.BlockSpec((3, h, C), lambda k: (0, k, 0)), wspec, mspec, mspec],
            out_specs=[wspec, mspec, mspec])(self.G, self.R0, self.R1, self.R2, self.R3, self.Wold, self.m, self.v, self.W, self.mo, self.vo)
        src = self.W.at[l, x, y, z, c]
        self.start("az", [self.sems.copy(src, src, me.zk(k)) for k in (1, 2, 3)])
    def g1(self):
        me, h, l = self.me, self.r // 2, self.l
        x, y, z, c = me.x, me.y, me.z, me.c
        self.wait("az")
        A = self.W.at[l, x, y, :, c, pl.ds(0, h)]; B = self.W.at[l, x, y, :, c, pl.ds(h, h)]
        self.start("axy1", [self.sems.copy(A, A, me.yn()), self.sems.copy(B, B, me.xn())])
        F = self.W.at[l, x, y, :, c]
        self.start("ac0", [self.sems.copy(F, F, me.core())])
    def g2(self):
        me, h, l = self.me, self.r // 2, self.l
        x, y, z, c = me.x, me.y, me.z, me.c
        self.wait("axy1")
        cps = []
        for q in range(2):
            A = self.W.at[l, x, q, :, c, pl.ds(0, h)]; B = self.W.at[l, q, y, :, c, pl.ds(h, h)]
            cps += [self.sems.copy(A, A, me.xn()), self.sems.copy(B, B, me.yn())]
        self.start("axy2", cps)
        A = self.W.at[l, x, 1 - y, :, c, pl.ds(0, h)]; B = self.W.at[l, 1 - x, y, :, c, pl.ds(h, h)]
        self.start("ac1", [self.sems.copy(A, A, me.core()), self.sems.copy(B, B, me.core())])
    def g3(self):
        me, h, l = self.me, self.r // 2, self.l
        x, y, z, c = me.x, me.y, me.z, me.c
        self.wait("axy2")
        cps = []
        for q in range(2):
            A = self.W.at[l, 1 - x, q, :, c, pl.ds(0, h)]; B = self.W.at[l, q, 1 - y, :, c, pl.ds(h, h)]
            cps += [self.sems.copy(A, A, me.core()), self.sems.copy(B, B, me.core())]
        self.start("ac2", cps)
    def g4(self):
        for k in ("ac0", "ac1", "ac2"): self.wait(k)
        self.drain()

def buf_shapes(r, C):
    h = r // 2
    S = lambda *s: jax.ShapeDtypeStruct(s, bf16)
    return [S(2, 2, 4, r, C), S(2, 8, h, C), S(2, 8, h, C), S(2, 4, h, C), S(2, 4, h, C), S(3, r, C), S(3, r, C)]
NB = 7


NAMES = ("w_gate", "w_up", "w_down")
ORDER = ((1, 2), (1, 0), (1, 1), (0, 2), (0, 0), (0, 1))
STAGES = ("s0", "s1", "s2", "s3", "s4", "g1", "g2", "g3", "g4")


def matmul(a, w):
    return jnp.dot(a, w, preferred_element_type=jnp.float32).astype(jnp.bfloat16)


def normed(h):
    wide = h.astype(jnp.float32)
    scale = lax.rsqrt(jnp.mean(wide**2, -1, keepdims=True) + 1e-6)
    return (wide * scale).astype(jnp.bfloat16)


def layer(h, w):
    a = normed(h)
    gate = jnp.dot(a, w["w_gate"], preferred_element_type=jnp.float32)
    up = jnp.dot(a, w["w_up"], preferred_element_type=jnp.float32)
    return h + matmul((jax.nn.silu(gate) * up).astype(jnp.bfloat16), w["w_down"])


def skew_order(count, lag):
    order = []
    for t in range(lag * count + len(STAGES)):
        for u in range(count):
            if 0 <= t - lag * u < len(STAGES):
                order.append((u, STAGES[t - lag * u]))
    return order


def kernel(sizes, order, *refs):
    n = len(ORDER)
    G, Wold, M, V, o = refs[:n], refs[n : n + 3], refs[n + 3 : n + 6], refs[n + 6 : n + 9], refs[n + 9 :]
    Wn, Mo, Vo, bufs, (ssem, rsem) = o[:3], o[3:6], o[6:9], o[9 : 9 + NB * n], o[9 + NB * n :]
    me = Me()
    barrier(me)
    sems = Sems(ssem, rsem)
    units = [
        Unit(me, sems, l, *sizes[w], G[i], Wold[w], M[w], V[w], Wn[w], Mo[w], Vo[w], bufs[NB * i : NB * i + NB])
        for i, (l, w) in enumerate(ORDER)
    ]
    for u, s in order:
        getattr(units[u], s)()


def communicate(sizes, layers, *args):
    hbm = pl.BlockSpec(memory_space=pl.ANY)
    outs = [jax.ShapeDtypeStruct((layers, 2, 2, 4, 2, r, C), bf16) for r, C in sizes]
    outs += [jax.ShapeDtypeStruct((layers, r, C), f32) for r, C in sizes] * 2
    for _, w in ORDER:
        outs += buf_shapes(*sizes[w])
    count = 27 * len(ORDER)
    return pl.pallas_call(
        functools.partial(kernel, sizes, skew_order(len(ORDER), 1)),
        out_shape=outs,
        in_specs=[hbm] * len(args),
        out_specs=[hbm] * len(outs),
        scratch_shapes=[pltpu.SemaphoreType.DMA((count,)), pltpu.SemaphoreType.DMA((count,))],
        compiler_params=pltpu.CompilerParams(collective_id=0, has_side_effects=True, vmem_limit_bytes=60 << 20),
    )(*args)


def solution(mesh):
    def step(x, dy, *arrays):
        weights, m, v = (arrays[i : i + 3] for i in (0, 3, 6))
        x, dy = x[0], dy[0]
        layers = weights[0].shape[0]
        sizes = [t.shape[1:] for t in m]
        per_layer = [{name: w[number] for name, w in zip(NAMES, weights, strict=True)} for number in range(layers)]

        def stack(per_layer):
            h = x
            for w in per_layer:
                h = layer(h, w)
            return h

        _, back = jax.vjp(stack, per_layer)
        grads = back(dy)[0]
        gs = [grads[l][NAMES[w]].reshape(2, 2, 4, 2, *sizes[w]) for l, w in ORDER]
        ws = [w.reshape(layers, 2, 2, 4, 2, *s) for w, s in zip(weights, sizes, strict=True)]
        out = communicate(sizes, layers, *gs, *ws, *m, *v)
        return tuple(w.reshape(t.shape) for w, t in zip(out[:3], weights, strict=True)) + tuple(out[3:9])

    whole, rows, seq = P(None, None, None), P(None, "dp", None), P(("rep", "dp"), None, None)
    return jax.shard_map(
        step,
        mesh=mesh,
        in_specs=(seq, seq) + (whole,) * 3 + (rows,) * 6,
        out_specs=(P("rep", None, None),) * 3 + (P("rep", "dp", None),) * 6,
        check_vma=False,
    )
```

time: 1800 us -> 1170 us (0.65)
  waiting for transfers between devices: 1100 us -> 0 us
  Pallas kernels: 0 us -> 563 us
  other arithmetic: 78.2 us -> 9.31 us
    reduce_scatter x6 -> x0, waiting for transfers between devices: 615 us -> none  [step(): lax.psum_scatter(grads[number][name], 'dp', scatter_dimension=0, tiled=True)]
    pallas_call x0 -> x1, Pallas kernels: none -> 563 us  [communicate(): pl.pallas_call(functools.partial(kernel, sizes, skew_order(len(ORDER), 1)...]
    all_gather x6 -> x0, waiting for transfers between devices: 480 us -> none  [step(): new[name][number] = (lax.all_gather(w, 'dp', axis=0, tiled=True), nm, nv)]
    another operation x6 -> x0, other arithmetic: 58.1 us -> none  [step(): jnp.stack([new[name][number][which] for number in range(layers)])]
    slice x3 -> x0, local copies, waits for them, and re-layouts: 48.7 us -> none  [the longest x2 32.3 us: step(): w[number]]
    unnamed x26 -> x47, local copies, waits for them, and re-layouts: 15.5 us -> 62.8 us
  transfers between devices with their start and end apart: 12 -> 0, of which waited for: 11 -> 0; matrix products, arithmetic and copies ran while one was open for 21% -> 0% of each run, Pallas kernels for 0% -> 0%
where the time goes in v2:
time: 1170 us; the launch traced here: 1160 us
  Pallas kernels  563 us (48%)
  matrix products  521 us (45%)
  local copies, waits for them, and re-layouts  62.8 us (5%)
    pallas_call x1, Pallas kernels, communicate(): pl.pallas_call(functools.partial(kernel, sizes, skew_order(len(ORDER), 1)...  563 us
    dot_general x5, matrix products, layer(): gate = jnp.dot(a, w['w_gate'], preferred_element_type=jnp.float32)  189 us
    dot_general x5, matrix products, layer(): up = jnp.dot(a, w['w_up'], preferred_element_type=jnp.float32)  177 us
    dot_general x5, matrix products, matmul(): jnp.dot(a, w, preferred_element_type=jnp.float32).astype(jnp.bfloat16)  155 us
    unnamed x47, local copies, waits for them, and re-layouts  62.8 us

profile of v2, /device:TPU:0, one launch (start us, length us, event | category | flops | bytes accessed | tf_op | source)
XLA Modules:
  0.0 1158.1 jit_solution(2177388723700178372)
XLA Ops:
  0.6 6.5 copy.20
  7.1 3.1 fusion.45
  10.2 0.0 copy-start.11
  10.2 29.8 %fusion.28 = f32[2048,5120]{1,0:T(8,128)} fusion(bf16[2,1024,5120]{2,1,0:T(8,128)(2,1)} %param.13, bf16[1,2048,1024]{2,1,0:T(8,128)(2,1)} %param.11, f32[2048]{0:T(1024)S(1)} %add_rsqrt_fusion), kind=kOutput, calls=%fused_computation.46 | convolution fusion | flops 21481127936 | bytes 56631296 | tf_op jit(solution)/shard_map/jvp()/dot_general | solution.py:194
  40.0 0.0 copy-done.11
  40.0 49.5 %multiply_convert_fusion.1 = (bf16[2048,5120]{1,0:T(8,128)(2,1)}, f32[2048,5120]{1,0:T(8,128)}) fusion(f32[2048,5120]{1,0:T(8,128)} %fusion.28, bf16[2,1024,5120]{2,1,0:T(8,128)(2,1)} %param.14, bf16[1,2048,1024]{2,1,0:T(8,128)(2,1)} %param.11, f32[2048]{0:T(1024)S(1)} %add_rsqrt_fusion), kind=kOutput, calls=%fused_computation.17 | convolution fusion | flops 21544042496 | bytes 119545856 | tf_op jit(solution)/shard_map/jvp()/dot_general | solution.py:195
  89.5 30.0 %fusion.49 = (f32[2048]{0:T(1024)S(1)}, bf16[2048,1024]{0,1:T(8,128)(2,1)}) fusion(bf16[2048,5120]{1,0:T(8,128)(2,1)} %get-tuple-element.27, bf16[2,5120,1024]{2,1,0:T(8,128)(2,1)} %param.15, bf16[1,2048,1024]{1,2,0:T(8,128)(2,1)} %copy.20), kind=kOutput, calls=%fused_computation.67 | convolution fusion | flops 21485320192 | bytes 39854080 | tf_op jit(solution)/shard_map/jvp()/dot_general | solution.py:183
  119.5 0.0 copy-start.9
  119.5 29.8 %fusion.17 = f32[2048,5120]{1,0:T(8,128)} fusion(bf16[2,1024,5120]{2,1,0:T(8,128)(2,1)} %param.14, bf16[2048,1024]{0,1:T(8,128)(2,1)} %get-tuple-element.30, f32[2048]{0:T(1024)S(1)} %fusion.69), kind=kOutput, calls=%fused_computation.35 | convolution fusion | flops 21481127936 | bytes 56631296 | tf_op jit(solution)/shard_map/jvp()/dot_general | solution.py:195
  149.2 0.0 copy-done.9
  149.2 30.2 %convolution_convert_fusion.1 = bf16[2048,5120]{1,0:T(8,128)(2,1)} fusion(bf16[2,5120,1024]{2,1,0:T(8,128)(2,1)} %param.15, bf16[1,2048,1024]{2,1,0:T(8,128)(2,1)} %param.12), kind=kOutput, calls=%fused_computation.25 | convolution fusion | flops 21485322240 | bytes 35651584 | tf_op jit(solution)/shard_map/transpose(jvp())/dot_general | solution.py:183
  179.4 57.3 %fusion.2 = (bf16[2048,5120]{1,0:T(8,128)(2,1)}, f32[2048,5120]{1,0:T(8,128)}) fusion(f32[2048,5120]{1,0:T(8,128)} %fusion.17, bf16[2048,5120]{1,0:T(8,128)(2,1)} %convolution_convert_fusion.1, bf16[2,1024,5120]{2,1,0:T(8,128)(2,1)} %param.13, bf16[2048,1024]{0,1:T(8,128)(2,1)} %get-tuple-element.30, f32[2048]{0:T(1024)S(1)} %fusion.69), kind=kOutput, calls=%fused_computation.8 | convolution fusion | flops 21606957056 | bytes 140517376 | tf_op jit(solution)/shard_map/jvp()/dot_general | solution.py:194
  236.7 37.1 %fusion.33 = bf16[5120,1024]{1,0:T(8,128)(2,1)} fusion(f32[2048,5120]{1,0:T(8,128)} %fusion.17, bf16[1,2048,1024]{2,1,0:T(8,128)(2,1)} %param.12, f32[2048,5120]{1,0:T(8,128)} %get-tuple-element.32), kind=kOutput, calls=%fused_computation.51 | convolution fusion | flops 21542993920 | bytes 98566144 | tf_op jit(solution)/shard_map/transpose(jvp())/dot_general | solution.py:183
  273.9 27.7 %convolution_convert_fusion.3 = bf16[1024,5120]{1,0:T(8,128)(2,1)} fusion(bf16[2048,5120]{1,0:T(8,128)(2,1)} %get-tuple-element.31, bf16[2048,1024]{0,1:T(8,128)(2,1)} %get-tuple-element.30, f32[2048]{0:T(1024)S(1)} %fusion.69), kind=kOutput, calls=%fused_computation.56 | convolution fusion | flops 21481127936 | bytes 35659776 | tf_op jit(solution)/shard_map/transpose(jvp())/dot_general | solution.py:194
  301.5 32.7 %fusion.34 = bf16[1024,5120]{1,0:T(8,128)(2,1)} fusion(bf16[2048,5120]{1,0:T(8,128)(2,1)} %convolution_convert_fusion.1, bf16[2048,1024]{0,1:T(8,128)(2,1)} %get-tuple-element.30, f32[2048]{0:T(1024)S(1)} %fusion.69, f32[2048,5120]{1,0:T(8,128)} %get-tuple-element.32), kind=kOutput, calls=%fused_computation.52 | convolution fusion | flops 21549285376 | bytes 77602816 | tf_op jit(solution)/shard_map/transpose(jvp())/dot_general | solution.py:195
  334.2 0.0 copy-start.1
  334.3 32.5 %fusion.11 = bf16[2048,1024]{0,1:T(8,128)(2,1)} fusion(bf16[2048,5120]{1,0:T(8,128)(2,1)} %convolution_convert_fusion.1, bf16[2,1024,5120]{2,1,0:T(8,128)(2,1)} %param.14, f32[2048,5120]{1,0:T(8,128)} %get-tuple-element.32), kind=kOutput, calls=%fused_computation.20 | convolution fusion | flops 21537751040 | bytes 77594624 | tf_op jit(solution)/shard_map/transpose(jvp())/dot_general | solution.py:195
  366.8 0.0 copy-done.1
  366.8 0.0 copy-start.10
  366.8 30.3 %fusion.51 = (f32[2048]{0:T(1024)S(1)}, bf16[2048,1024]{0,1:T(8,128)(2,1)}) fusion(bf16[2048,1024]{0,1:T(8,128)(2,1)S(1)} %copy-done.1, bf16[2048,1024]{0,1:T(8,128)(2,1)} %fusion.11, bf16[2048,5120]{1,0:T(8,128)(2,1)} %get-tuple-element.31, bf16[2,1024,5120]{2,1,0:T(8,128)(2,1)} %param.13), kind=kOutput, calls=%fused_computation.69 | convolution fusion | flops 21485320192 | bytes 44048384 | tf_op jit(solution)/shard_map/transpose(jvp())/dot_general | solution.py:194
  397.1 6.4 copy.21
  403.5 0.0 copy-done.10
  403.6 6.2 fusion.54
  409.8 0.0 copy-start.2
  409.8 28.3 %convolution_convert_fusion.2 = bf16[5120,1024]{1,0:T(8,128)(2,1)} fusion(bf16[2048,5120]{1,0:T(8,128)(2,1)} %get-tuple-element.27, bf16[2048,1024]{0,1:T(8,128)(2,1)S(1)} %fusion.54), kind=kOutput, calls=%fused_computation.55 | convolution fusion | flops 21480079360 | bytes 35651584 | tf_op jit(solution)/shard_map/transpose(jvp())/dot_general | solution.py:183
  438.1 0.0 copy-done.2
  438.1 0.0 copy-start.12
  438.1 29.4 %convolution_convert_fusion = bf16[2048,5120]{1,0:T(8,128)(2,1)} fusion(bf16[2048,1024]{0,1:T(8,128)(2,1)} %copy-done.2, bf16[2,5120,1024]{2,1,0:T(8,128)(2,1)} %param.15), kind=kOutput, calls=%fused_computation.24 | convolution fusion | flops 21485322240 | bytes 35651584 | tf_op jit(solution)/shard_map/transpose(jvp())/dot_general | solution.py:183
  467.5 0.0 copy-done.12
  467.5 44.2 %fusion.35 = bf16[1024,5120]{1,0:T(8,128)(2,1)} fusion(f32[2048,5120]{1,0:T(8,128)} %fusion.28, f32[2048,5120]{1,0:T(8,128)} %get-tuple-element.28, bf16[2048,5120]{1,0:T(8,128)(2,1)} %convolution_convert_fusion, bf16[1,2048,1024]{1,2,0:T(8,128)(2,1)} %copy.20, f32[2048]{0:T(1024)S(1)} %copy-done.12), kind=kOutput, calls=%fused_computation.53 | convolution fusion | flops 21601714176 | bytes 119545856 | tf_op jit(solution)/shard_map/transpose(jvp())/dot_general | solution.py:194
  511.7 32.6 %fusion.38 = bf16[1024,5120]{1,0:T(8,128)(2,1)} fusion(bf16[2048,5120]{1,0:T(8,128)(2,1)} %convolution_convert_fusion, f32[2048,5120]{1,0:T(8,128)} %fusion.28, bf16[1,2048,1024]{1,2,0:T(8,128)(2,1)} %copy.20, f32[2048]{0:T(1024)S(1)} %copy-done.12), kind=kOutput, calls=%fused_computation.54 | convolution fusion | flops 21549285376 | bytes 77602816 | tf_op jit(solution)/shard_map/transpose(jvp())/dot_general | solution.py:195
  544.3 563.5 %shard_map.178 = (bf16[2,2,2,4,2,32,5120]{6,5,4,3,2,1,0:T(8,128)(2,1)}, bf16[2,2,2,4,2,32,5120]{6,5,4,3,2,1,0:T(8,128)(2,1)}, bf16[2,2,2,4,2,160,1024]{6,5,4,3,2...) custom-call(bf16[2,2,4,2,160,1024]{5,4,3,2,1,0:T(8,128)(2,1)} %bitca, ...), custom_call_target="tpu_custom_call" | custom-call | tf_op jit(solution)/shard_map/pallas_call | solution.py:230
  1107.8 0.0 copy-start
  1107.8 0.0 slice-start
  1107.8 0.0 slice-start.1
  1107.8 0.0 slice-start.2
  1107.8 21.0 %copy.31 = bf16[2,1024,5120]{2,1,0:T(8,128)(2,1)} copy(bf16[2,1024,5120]{2,1,0:T(8,128)(2,1)} %bitcast.84) | data formatting | bytes 41943040
  1128.7 0.0 copy-done
  1128.8 0.0 slice-start.4
  1128.8 10.6 copy.32
  1139.4 0.0 slice-done
  1139.4 0.0 slice-done.1
  1139.4 0.0 slice-done.2
  1139.4 1.9 slice-done.3
  1141.3 1.2 slice-done.4
  1142.5 0.0 copy-start.8
  1142.5 0.0 copy-start.7
  1142.5 0.0 copy-start.6
  1142.5 0.0 copy-start.5
  1142.5 8.8 copy.33
  1151.3 0.0 copy-done.8
  1151.3 0.0 copy-start.4
  1151.3 0.0 copy-start.3
  1151.3 1.1 copy.34
  1152.3 0.0 copy-done.7
  1152.3 1.1 copy.35
  1153.4 0.0 copy-done.6
  1153.4 1.1 copy.36
  1154.5 0.0 copy-done.5
  1154.5 1.1 copy.37
  1155.5 0.0 copy-done.4
  1155.5 1.1 copy.38
  1156.6 0.0 copy-done.3
  1156.6 1.1 copy.39
  (5 shorter events, 0.0 us)
Async XLA Ops:
  10.2 29.8 %copy-start.11 = (f32[2048]{0:T(1024)}, f32[2048]{0:T(1024)S(1)}, u32[]{:S(2)}) copy-start(f32[2048]{0:T(1024)S(1)} %add_rsqrt_fusion) | copy-start | bytes 24580
  119.5 29.8 %copy-start.9 = (f32[2048]{0:T(1024)}, f32[2048]{0:T(1024)S(1)}, u32[]{:S(2)}) copy-start(f32[2048]{0:T(1024)S(1)} %get-tuple-element.29) | copy-start | bytes 24580
  334.2 32.5 %copy-start.1 = (bf16[2048,1024]{0,1:T(8,128)(2,1)S(1)}, bf16[2048,1024]{0,1:T(8,128)(2,1)}, u32[]{:S(2)}) copy-start(bf16[2048,1024]{0,1:T(8,128)(2,1)} %get-tuple-element.30) | copy-start | bytes 12582916
  366.8 36.7 %copy-start.10 = (f32[2048]{0:T(1024)S(1)}, f32[2048]{0:T(1024)}, u32[]{:S(2)}) copy-start(f32[2048]{0:T(1024)} %copy-done.9) | copy-start | bytes 24580
  409.8 28.4 %copy-start.2 = (bf16[2048,1024]{0,1:T(8,128)(2,1)}, bf16[2048,1024]{0,1:T(8,128)(2,1)S(1)}, u32[]{:S(2)}) copy-start(bf16[2048,1024]{0,1:T(8,128)(2,1)S(1)} %fusion.54) | copy-start | bytes 12582916
  438.1 29.4 %copy-start.12 = (f32[2048]{0:T(1024)S(1)}, f32[2048]{0:T(1024)}, u32[]{:S(2)}) copy-start(f32[2048]{0:T(1024)} %copy-done.11) | copy-start | bytes 24580
  1107.8 21.0 %copy-start = (bf16[2,2,2,4,2,32,5120]{6,5,4,3,2,1,0:T(8,128)(2,1)S(1)}, bf16[2,2,2,4,2,32,5120]{6,5,4,3,2,1,0:T(8,128)(2,1)}, u32[]{:S(2)}) copy-start(bf16[2,2,2,4,2,32,5120]{6,5,4,3,2,1,0:T(8,128)(2,1)} %get-tuple-element.19) | copy-start | bytes 62914564
  1107.8 31.6 %slice-start = ((s8[20971520]{0:T(1024)(128)(4,1)}), s8[4194304]{0:T(1024)(128)(4,1)S(1)}, s32[]{:S(2)}) async-start(s8[20971520]{0:T(1024)(128)(4,1)} %bitcast.80), calls=%async_computation | async-start | bytes 8388608
  1107.8 31.6 %slice-start.1 = ((s8[20971520]{0:T(1024)(128)(4,1)}), s8[4194304]{0:T(1024)(128)(4,1)S(1)}, s32[]{:S(2)}) async-start(s8[20971520]{0:T(1024)(128)(4,1)} %bitcast.80), calls=%async_computation.1 | async-start | bytes 8388608
  1107.8 31.6 %slice-start.2 = ((s8[20971520]{0:T(1024)(128)(4,1)}), s8[4194304]{0:T(1024)(128)(4,1)S(1)}, s32[]{:S(2)}) async-start(s8[20971520]{0:T(1024)(128)(4,1)} %bitcast.80), calls=%async_computation.2 | async-start | bytes 8388608
  1128.8 12.5 %slice-start.3 = ((s8[20971520]{0:T(1024)(128)(4,1)}), s8[4194304]{0:T(1024)(128)(4,1)S(1)}, s32[]{:S(2)}) async-start(s8[20971520]{0:T(1024)(128)(4,1)} %bitcast.80), calls=%async_computation.3 | async-start | bytes 8388608
  1128.8 13.7 %slice-start.4 = ((s8[20971520]{0:T(1024)(128)(4,1)}), s8[4194304]{0:T(1024)(128)(4,1)S(1)}, s32[]{:S(2)}) async-start(s8[20971520]{0:T(1024)(128)(4,1)} %bitcast.80), calls=%async_computation.4 | async-start | bytes 8388608
  1142.5 8.8 copy-start.8
  1142.5 9.9 copy-start.7
  1142.5 10.9 copy-start.6
  1142.5 12.0 %copy-start.5 = (f32[2,32,5120]{2,1,0:T(8,128)S(1)}, f32[2,32,5120]{2,1,0:T(8,128)}, u32[]{:S(2)}) copy-start(f32[2,32,5120]{2,1,0:T(8,128)} %get-tuple-element.50) | copy-start | bytes 3932164
  1151.3 4.2 copy-start.4
  1151.3 5.3 copy-start.3

commit v3 on v1

v3 whole, which is shorter than its diff:
```python
import functools

import jax
import jax.numpy as jnp
from jax import lax
from jax.experimental import pallas as pl
from jax.experimental.pallas import tpu as pltpu
from jax.sharding import PartitionSpec as P

MESH = pl.DeviceIdType.MESH
f32, bf16 = jnp.float32, jnp.bfloat16
T, D, F, LAYERS = 2048, 1024, 5120, 2
TILE = 256
STEPS = F // TILE
CHUNK = 5
PIECES = STEPS // CHUNK
WIDE = CHUNK * TILE
VMEM_LIMIT = 63 << 20
NT = (((1,), (1,)), ((), ()))
TN = (((0,), (0,)), ((), ()))


def dot(a, b):
    return jnp.dot(a, b, preferred_element_type=f32)


def dot_nt(a, b):
    return lax.dot_general(a, b, NT, preferred_element_type=f32)


def dot_tn(a, b):
    return lax.dot_general(a, b, TN, preferred_element_type=f32)


def normed(h):
    wide = h.astype(f32)
    scale = lax.rsqrt(jnp.mean(wide**2, -1, keepdims=True) + 1e-6)
    return (wide * scale).astype(bf16)


def up_kernel(x, wg, wu, a_out, act, a_scr):
    @pl.when(pl.program_id(0) == 0)
    def _():
        @pl.loop(0, T // 256)
        def _(m):
            s = pl.ds(m * 256, 256)
            a = normed(x[s, :])
            a_scr[s, :] = a
            a_out[s, :] = a

    def rows(m, _):
        s = pl.ds(m * 512, 512)
        gate, up = dot(a_scr[s, :], wg[...]), dot(a_scr[s, :], wu[...])
        act[s, :] = (jax.nn.silu(gate) * up).astype(bf16)
        return 0

    lax.fori_loop(0, T // 512, rows, 0, unroll=4)


def down_kernel(x, act, wd, h_out, a_out):
    h = x[...] + dot(act[...], wd[...]).astype(bf16)
    h_out[...] = h
    a_out[...] = normed(h)


def forward(x, wg, wu, wd):
    params = pltpu.CompilerParams(vmem_limit_bytes=VMEM_LIMIT)
    full = pl.BlockSpec((T, D), lambda j: (0, 0))
    columns = pl.BlockSpec((None, D, 512), lambda j: (0, 0, j))
    state, hidden = jax.ShapeDtypeStruct((T, D), bf16), jax.ShapeDtypeStruct((T, F), bf16)
    a0, act0 = pl.pallas_call(
        up_kernel,
        grid=(F // 512,),
        in_specs=[full, columns, columns],
        out_specs=[full, pl.BlockSpec((T, 512), lambda j: (0, j))],
        out_shape=[state, hidden],
        scratch_shapes=[pltpu.VMEM((T, D), bf16)],
        compiler_params=params,
        name="up",
    )(x, wg, wu)
    row = pl.BlockSpec((256, D), lambda m: (m, 0))
    whole = pl.BlockSpec((None, F, D), lambda m: (0, 0, 0), pipeline_mode=pl.Buffered(1))
    h1, a1 = pl.pallas_call(
        down_kernel,
        grid=(T // 256,),
        in_specs=[row, pl.BlockSpec((256, F), lambda m: (m, 0)), whole],
        out_specs=[row, row],
        out_shape=[state, state],
        compiler_params=params,
        name="down",
    )(x, act0, wd)
    return a0, act0, h1, a1


def index(x, y, z, c):
    return ((x * 2 + y) * 4 + z) * 2 + c


class Me:
    def __init__(self):
        d = lax.axis_index("dp")
        self.c = lax.rem(d, 2)
        self.z = lax.rem(lax.div(d, 2), 4)
        self.y = lax.rem(lax.div(d, 8), 2)
        self.x = lax.div(d, 16)
        self.core = index(self.x, self.y, self.z, 1 - self.c)
        self.xn = index(1 - self.x, self.y, self.z, self.c)
        self.yn = index(self.x, 1 - self.y, self.z, self.c)
        self.zn = {k: index(self.x, self.y, lax.rem(self.z + k, 4), self.c) for k in (1, 2, 3)}


def barrier(me):
    sem = pltpu.get_barrier_semaphore()
    peers = [me.core, me.xn, me.yn, *me.zn.values()]
    for peer in peers:
        pl.semaphore_signal(sem, inc=1, device_id=(0, peer), device_id_type=MESH)
    pl.semaphore_wait(sem, len(peers))


def pick(k, a, b):
    return (1 - k) * a + k * b


STAGES = ("s0", "s1", "s2", "s3", "s4", "g1", "g2", "g3", "g4")
KEYS = ("core", "xy1", "xy2", "z", "az", "axy1", "ac0", "axy2", "ac1", "ac2")


class Piece:
    def __init__(self, me, sems, layer, r, C, G, bufs, parts, tmp):
        self.me, self.l, self.r, self.C, self.G, self.parts, self.tmp = me, layer, r, C, G, parts, tmp
        self.R0, self.S0, self.R1, self.S1, self.R2, self.S2, self.R3 = bufs
        self.sems = {key: sems.take() for key in KEYS}

    def pairs(self, key):
        me, h = self.me, self.r // 2
        x, y, z, c = me.x, me.y, me.z, me.c
        if key == "core":
            return [(self.G.at[:, :, :, 1 - c], self.R0, me.core)]
        if key == "xy1":
            return [(self.S0.at[0], self.R1.at[0], me.xn), (self.S0.at[1], self.R1.at[1], me.yn)]
        if key == "xy2":
            return [(self.S1.at[0], self.R2.at[0], me.yn), (self.S1.at[1], self.R2.at[1], me.xn)]
        if key == "z":
            return [(self.S2.at[lax.rem(z + k, 4)], self.R3.at[k - 1], me.zn[k]) for k in (1, 2, 3)]
        out = []
        for part in self.parts:
            cols = pl.ds(part["block"] * part["width"], part["width"])
            lo, hi, both = pl.ds(0, h), pl.ds(h, h), pl.ds(0, self.r)

            def w(a, b, d, rows):
                return part["W"].at[self.l, a, b, d, c, rows, cols]

            every = slice(None)
            if key == "az":
                spots = [(w(x, y, z, both), me.zn[k]) for k in (1, 2, 3)]
            elif key == "axy1":
                spots = [(w(x, y, every, lo), me.yn), (w(x, y, every, hi), me.xn)]
            elif key == "ac0":
                spots = [(w(x, y, every, both), me.core)]
            elif key == "axy2":
                spots = [(w(x, every, every, lo), me.xn), (w(every, y, every, hi), me.yn)]
            elif key == "ac1":
                spots = [(w(x, 1 - y, every, lo), me.core), (w(1 - x, y, every, hi), me.core)]
            else:
                spots = [(w(1 - x, every, every, lo), me.core), (w(every, 1 - y, every, hi), me.core)]
            out += [(ref, ref, dev) for ref, dev in spots]
        return out

    def start(self, *keys):
        for key in keys:
            send, recv = self.sems[key]
            for src, dst, dev in self.pairs(key):
                pltpu.make_async_remote_copy(src_ref=src, dst_ref=dst, send_sem=send, recv_sem=recv, device_id=(0, dev), device_id_type=MESH).start()

    def whole(self, key):
        return {"core": self.R0, "z": self.R3, "az": self.R3, "xy1": self.R1, "axy2": self.R1, "ac2": self.R1}.get(key, self.R2)

    def wait(self, *keys, which=1):
        for key in keys:
            pltpu.make_async_copy(self.whole(key), self.whole(key), self.sems[key][which]).wait()

    def half(self, k):
        return pl.ds(k * (self.r // 2), self.r // 2)

    def add(self, terms, outs, key):
        V, sem = self.tmp["V"], self.tmp["sem"]
        n, flat = len(terms[0]), len(terms[0][0].shape) == 3
        a, b = (1, terms[0][0].shape[0]) if flat else terms[0][0].shape[:2]

        def view(i, k):
            return V.at[i, k, 0] if flat else V.at[i, k]

        for k in range(2):
            for i, term in enumerate(terms[k]):
                pltpu.make_async_copy(term, view(i, k), sem.at[k]).start()
        for k in range(2):
            all_of = V.at[pl.ds(0, n), k, pl.ds(0, a)]
            pltpu.make_async_copy(all_of, all_of, sem.at[k]).wait()

            @pl.loop(0, a * b)
            def _(j):
                q, d = j // b, lax.rem(j, b)
                total = V[0, k, q, d].astype(f32)
                for i in range(1, n):
                    total = total + V[i, k, q, d].astype(f32)
                V[4, k, q, d] = total.astype(bf16)

            pltpu.make_async_copy(view(4, k), outs[k], sem.at[2 + k]).start()
        for k in range(2):
            pltpu.make_async_copy(view(4, k), outs[k], sem.at[2 + k]).wait()
        self.start(key)

    def s0(self):
        self.start("core")

    def s1(self):
        me = self.me
        self.wait("core")
        G, R0, lo, hi = self.G, self.R0, self.half(0), self.half(1)
        self.add(
            [
                [G.at[1 - me.x, :, :, me.c, lo], R0.at[1 - me.x, :, :, lo]],
                [G.at[:, 1 - me.y, :, me.c, hi], R0.at[:, 1 - me.y, :, hi]],
            ],
            [self.S0.at[0], self.S0.at[1]],
            "xy1",
        )

    def s2(self):
        me = self.me
        self.wait("xy1")
        G, R0, R1, lo, hi = self.G, self.R0, self.R1, self.half(0), self.half(1)
        self.add(
            [
                [G.at[me.x, 1 - me.y, :, me.c, lo], R0.at[me.x, 1 - me.y, :, lo], R1.at[0, 1 - me.y]],
                [G.at[1 - me.x, me.y, :, me.c, hi], R0.at[1 - me.x, me.y, :, hi], R1.at[1, 1 - me.x]],
            ],
            [self.S1.at[0], self.S1.at[1]],
            "xy2",
        )

    def s3(self):
        me = self.me
        self.wait("xy2")
        x, y = me.x, me.y
        self.add(
            [
                [self.G.at[x, y, :, me.c, self.half(k)], self.R0.at[x, y, :, self.half(k)], self.R1.at[k, (y, x)[k]], self.R2.at[k]]
                for k in range(2)
            ],
            [self.S2.at[:, self.half(0)], self.S2.at[:, self.half(1)]],
            "z",
        )

    def s4(self):
        me, l, h = self.me, self.l, self.r // 2
        x, y, z, c = me.x, me.y, me.z, me.c
        self.wait("z")
        B, A, sem = self.tmp["B"], self.tmp["A"], self.tmp["sem"]
        width = self.C // len(self.parts)
        lo, hi = self.half(0), self.half(1)
        terms = [(self.G.at[x, y, z, c], B.at[0]), (self.R0.at[x, y, z], B.at[1]), (self.R3, B.at[pl.ds(4, 3)])]
        terms += [(self.R1.at[0, y, z], B.at[2, lo]), (self.R1.at[1, x, z], B.at[2, hi])]
        terms += [(self.R2.at[0, z], B.at[3, lo]), (self.R2.at[1, z], B.at[3, hi])]
        moments, w_out, out = [], [], []
        for p, part in enumerate(self.parts):
            there, here = pl.ds(part["block"] * width, width), pl.ds(p * width, width)
            terms += [(part["w"].at[l, x, y, z, c, :, there], B.at[7, :, here])]
            moments += [(part["m"].at[l, :, there], A.at[0, :, here]), (part["v"].at[l, :, there], A.at[1, :, here])]
            w_out += [(B.at[8, :, here], part["W"].at[l, x, y, z, c, :, there])]
            out += [(A.at[2, :, here], part["M"].at[l, :, there]), (A.at[3, :, here], part["V"].at[l, :, there])]

        def begin(pairs, i):
            for src, dst in pairs:
                pltpu.make_async_copy(src, dst, sem.at[i]).start()

        def end(ref, i):
            pltpu.make_async_copy(ref, ref, sem.at[i]).wait()

        begin(terms, 0)
        begin(moments, 1)
        end(B.at[pl.ds(0, 8)], 0)
        end(A.at[pl.ds(0, 2)], 1)
        blocks, across = self.r // 16, self.C // 512

        @pl.loop(0, blocks * across)
        def _(j):
            rows = pl.ds(pl.multiple_of(lax.rem(j, blocks) * 16, 16), 16)
            cols = pl.ds(pl.multiple_of(j // blocks * 512, 512), 512)
            t = B[0, rows, cols].astype(f32)
            for i in range(1, 7):
                t = t + B[i, rows, cols].astype(f32)
            t = t.astype(bf16).astype(f32)
            m = 0.9 * A[0, rows, cols] + 0.1 * t
            v = 0.95 * A[1, rows, cols] + 0.05 * t * t
            w = B[7, rows, cols].astype(f32)
            B[8, rows, cols] = (w - 0.02 * (m * lax.rsqrt(v + 1e-8) + 0.1 * w)).astype(bf16)
            A[2, rows, cols] = m
            A[3, rows, cols] = v

        begin(w_out, 2)
        begin(out, 3)
        end(B.at[8], 2)
        self.start("az")
        end(A.at[pl.ds(2, 2)], 3)

    def g1(self):
        self.wait("az")
        self.start("axy1", "ac0")

    def g2(self):
        self.wait("axy1")
        self.start("axy2", "ac1")

    def g3(self):
        self.wait("axy2")
        self.start("ac2")

    def g4(self):
        self.wait("ac0", "ac1", "ac2")
        self.wait(*KEYS, which=0)


class Sems:
    def __init__(self, send=None, recv=None):
        self.send, self.recv, self.n = send, recv, 0

    def take(self):
        self.n += 1
        return self.send.at[self.n - 1], self.recv.at[self.n - 1]


def buffers(r, C):
    h = r // 2
    shapes = (2, 2, 4, r, C), (2, 2, 4, h, C), (2, 2, 4, h, C), (2, 4, h, C), (2, 4, h, C), (4, r, C), (3, r, C)
    return [jax.ShapeDtypeStruct(s, bf16) for s in shapes]


HOSTS = (
    ("p1", 6.3, STEPS, [(CHUNK * (q + 1), [q]) for q in range(PIECES)]),
    ("p2", 3.1, 8, [(8, [4, 5])]),
    ("p3", 5.3, 10, []),
    ("p2", 3.1, 8, [(8, [6, 7])]),
    ("p1", 6.0, STEPS, [(CHUNK * (q + 1), [8 + q]) for q in range(PIECES)]),
)
COUNT = 12


def plan():
    cost = {"s0": 0.2, "s1": 3.6, "s2": 3.0, "s3": 2.9, "s4": 4.6, "g1": 0.2, "g2": 0.3, "g3": 0.3}
    links = {
        "s0": {"C": 5.2},
        "s1": {"X": 14.5, "Y": 14.5},
        "s2": {"X": 7.3, "Y": 7.3},
        "s3": {"Z": 14.5},
        "s4": {"Z": 14.5},
        "g1": {"X": 7.3, "Y": 7.3},
        "g2": {"X": 14.5, "Y": 14.5},
        "g3": {"C": 2.6},
    }
    now, free = 0.0, dict.fromkeys("XYZC", 0.0)
    done, ready = [0] * COUNT, [None] * COUNT
    last = len(STAGES) - 1

    def run(u):
        nonlocal now
        stage = STAGES[done[u]]
        now += cost[stage]
        end = now
        for link, span in links[stage].items():
            free[link] = max(now, free[link]) + span
            end = max(end, free[link])
        ready[u] = end + 2.5
        done[u] += 1
        return u, stage

    def candidates():
        c = [u for u in range(COUNT) if ready[u] is not None and done[u] < last and ready[u] <= now]
        return sorted(c, key=lambda u: (done[u] >= 4, u))

    schedule = []
    for _, span, steps, completes in HOSTS:
        slots = {}
        for s in range(steps):
            for at, pieces in completes:
                if at == s:
                    for u in pieces:
                        ready[u] = now
            while candidates():
                slots.setdefault(s, []).append(run(candidates()[0]))
            now += span
        for at, pieces in completes:
            if at == steps:
                for u in pieces:
                    ready[u] = now
        schedule.append(slots)
    tail = []
    while min(done) < last:
        u = (candidates() or [min((u for u in range(COUNT) if done[u] < last), key=lambda u: ready[u])])[0]
        now = max(now, ready[u])
        tail.append(run(u))
    return schedule, tail + [(u, "g4") for u in range(COUNT)]


def hidden_backward(layer, wg, wu, wd, keep, G, a_scr, dh_scr, gbuf, gsem, scratch, hook):
    def out_copies(i):
        q, col = i // CHUNK, lax.rem(i, CHUNK) * TILE
        return [
            pltpu.make_async_copy(gbuf.at[k], G.at[q, :, :, :, :, :, pl.ds(pl.multiple_of(k * WIDE + col, TILE), TILE)], gsem.at[k]) for k in range(2)
        ]

    def body(step, wg, wu, wd, *outs):
        i = step.index[0]
        act, dg, du = outs if keep else (None, *scratch)

        def rows(m, _):
            s = pl.ds(m * 512, 512)
            a = a_scr[s, :]
            gate, up, d = dot(a, wg[...]), dot(a, wu[...]), dot_nt(dh_scr[s, :], wd[...])
            d = d.astype(bf16).astype(f32)
            sig = 1.0 / (1.0 + jnp.exp(-gate))
            silu = gate * sig
            if keep:
                act[s, :] = (silu * up).astype(bf16)
            du[s, :] = (d * silu).astype(bf16)
            dg[s, :] = (d * up * (sig + silu * (1.0 - sig))).astype(bf16)
            return 0

        lax.fori_loop(0, T // 512, rows, 0, unroll=4)

        @pl.when(i > 0)
        def _():
            for copy in out_copies(i - 1):
                copy.wait()

        hook(i)
        gbuf[0] = dot_tn(a_scr[...], dg[...]).astype(bf16).reshape(gbuf.shape[1:])
        gbuf[1] = dot_tn(a_scr[...], du[...]).astype(bf16).reshape(gbuf.shape[1:])
        for copy in out_copies(i):
            copy.start()

    columns = pl.BlockSpec((None, D, TILE), lambda i: (layer, 0, i))
    tile = pl.BlockSpec((T, TILE), lambda i: (0, i))
    pltpu.emit_pipeline(
        body,
        grid=(STEPS,),
        in_specs=[columns, columns, pl.BlockSpec((None, TILE, D), lambda i: (layer, i, 0))],
        out_specs=[tile] * 3 if keep else [],
        _explicit_indices=True,
    )(wg, wu, wd, *(keep or ()))
    for copy in out_copies(STEPS - 1):
        copy.wait()


def down_gradient(act, Ga, Gb, dh_scr, hook):
    def body(step, act, ga, gb):
        hook(step.index[0])
        ga[...] = dot_tn(act[...], dh_scr[:, : D // 2]).astype(bf16).reshape(ga.shape)
        gb[...] = dot_tn(act[...], dh_scr[:, D // 2 :]).astype(bf16).reshape(gb.shape)

    out = pl.BlockSpec((None, None, 2, 2, 160, D // 2), lambda i: (i // 4, lax.rem(i // 2, 2), lax.rem(i, 2), 0, 0, 0))
    pltpu.emit_pipeline(
        body, grid=(8,), in_specs=[pl.BlockSpec((T, 640), lambda i: (0, i))], out_specs=[out, out], _explicit_indices=True
    )(act, Ga, Gb)


def state_gradient(layer, dg, du, wg, wu, acc, hook):
    def body(step, dg, du, wg, wu):
        i = step.index[0]
        hook(i)

        @pl.when(i == 0)
        def _():
            acc[...] = jnp.zeros_like(acc)

        for m in range(2):
            s = pl.ds(m * (T // 2), T // 2)
            acc[s, :] += dot_nt(dg[s, :], wg[...]) + dot_nt(du[s, :], wu[...])

    tile = pl.BlockSpec((T, 512), lambda i: (0, i))
    columns = pl.BlockSpec((None, D, 512), lambda i: (layer, 0, i))
    pltpu.emit_pipeline(body, grid=(F // 512,), in_specs=[tile, tile, columns, columns], _explicit_indices=True)(dg, du, wg, wu)


def through_norm(acc, h_scr, dh_scr):
    @pl.loop(0, T // 256)
    def _(m):
        s = pl.ds(m * 256, 256)
        da = acc[s, :].astype(bf16).astype(f32)
        wide = h_scr[s, :].astype(f32)
        scale = lax.rsqrt(jnp.mean(wide**2, -1, keepdims=True) + 1e-6)
        along = jnp.sum(da * wide, -1, keepdims=True) * (1.0 / D)
        d = da * scale - wide * (scale * scale * scale * along)
        dh_scr[s, :] = dh_scr[s, :] + d.astype(bf16)


def load(sems, *pairs):
    copies = [pltpu.make_async_copy(src, dst, sems.at[i]) for i, (src, dst) in enumerate(pairs)]
    for copy in copies:
        copy.start()
    for copy in copies:
        copy.wait()


def backward_kernel(sizes, *refs):
    (a0, act0, h1, a1, dy), w3, w7, m, v, refs = refs[:5], refs[5:8], refs[8:11], refs[11:14], refs[14:17], refs[17:]
    W, M, V, (act, dg, du), Gs, refs = refs[:3], refs[3:6], refs[6:9], refs[9:12], refs[12:18], refs[18:]
    bufs, refs = refs[: 7 * COUNT], refs[7 * COUNT :]
    send, recv, load_sem, gsem, work_sem, a_scr, dh_scr, acc, gbuf, dg_scr, du_scr, V_wide, B_wide, A_wide, V_down, B_down, A_down = refs
    G1, G1a, G1b, G0a, G0b, G0 = Gs
    me = Me()
    barrier(me)
    sems = Sems(send, recv)

    def part(i, block, width):
        return dict(w=w7[i], m=m[i], v=v[i], W=W[i], M=M[i], V=V[i], block=block, width=width)

    def piece(u, layer, r, C, G, parts, V, B, A):
        return Piece(me, sems, layer, r, C, G, bufs[7 * u : 7 * u + 7], parts, dict(V=V, B=B, A=A, sem=work_sem))

    def wide(u, layer, G, q):
        return piece(u, layer, sizes[0][0], 2 * WIDE, G.at[q], [part(0, q, WIDE), part(1, q, WIDE)], V_wide, B_wide, A_wide)

    def down(u, layer, G, q):
        return piece(u, layer, sizes[2][0], D // 2, G, [part(2, q, D // 2)], V_down, B_down, A_down)

    pieces = [wide(q, 1, G1, q) for q in range(4)] + [down(4, 1, G1a, 0), down(5, 1, G1b, 1)]
    pieces += [down(6, 0, G0a, 0), down(7, 0, G0b, 1)] + [wide(8 + q, 0, G0, q) for q in range(4)]
    schedule, tail = plan()

    def hook_of(host):
        def hook(i):
            for s, jobs in schedule[host].items():

                @pl.when(i == s)
                def _():
                    for u, stage in jobs:
                        getattr(pieces[u], stage)()

        return hook

    load(load_sem, (a1, a_scr), (dy, dh_scr))
    hidden_backward(1, *w3, (act, dg, du), G1, a_scr, dh_scr, gbuf, gsem, None, hook_of(0))
    down_gradient(act, G1a, G1b, dh_scr, hook_of(1))
    state_gradient(1, dg, du, w3[0], w3[1], acc, hook_of(2))
    load(load_sem, (h1, a_scr))
    through_norm(acc, a_scr, dh_scr)
    load(load_sem, (a0, a_scr))
    down_gradient(act0, G0a, G0b, dh_scr, hook_of(3))
    hidden_backward(0, *w3, None, G0, a_scr, dh_scr, gbuf, gsem, (dg_scr, du_scr), hook_of(4))
    for u, stage in tail:
        getattr(pieces[u], stage)()


def backward(sizes, a0, act0, h1, a1, dy, weights, m, v):
    hbm = pl.BlockSpec(memory_space=pl.ANY)

    def shape(s, dtype=bf16):
        return jax.ShapeDtypeStruct(s, dtype)

    views = [w.reshape(LAYERS, 2, 2, 4, 2, *s) for w, s in zip(weights, sizes, strict=True)]
    args = [a0, act0, h1, a1, dy, *weights, *views, *m, *v]
    outs = [shape(w.shape) for w in views] + [shape((LAYERS, *s), f32) for s in sizes] * 2 + [shape((T, F))] * 3
    wide, down = shape((PIECES, 2, 2, 4, 2, sizes[0][0], 2 * WIDE)), shape((2, 2, 4, 2, sizes[2][0], D // 2))
    outs += [wide, down, down, down, down, wide]
    for u in range(COUNT):
        outs += buffers(sizes[2][0], D // 2) if 4 <= u < 8 else buffers(sizes[0][0], 2 * WIDE)
    count = COUNT * len(KEYS)
    tokens = pltpu.VMEM((T, D), bf16)
    tile = pltpu.VMEM((T, TILE), bf16)

    def work(r, C):
        return pltpu.VMEM((5, 2, 2, 4, r // 2, C), bf16), pltpu.VMEM((9, r, C), bf16), pltpu.VMEM((4, r, C), f32)

    return pl.pallas_call(
        functools.partial(backward_kernel, sizes),
        out_shape=outs,
        in_specs=[hbm] * len(args),
        out_specs=[hbm] * len(outs),
        scratch_shapes=[
            pltpu.SemaphoreType.DMA((count,)),
            pltpu.SemaphoreType.DMA((count,)),
            pltpu.SemaphoreType.DMA((2,)),
            pltpu.SemaphoreType.DMA((2,)),
            pltpu.SemaphoreType.DMA((4,)),
            tokens,
            tokens,
            pltpu.VMEM((T, D), f32),
            pltpu.VMEM((2, 2, 2, 4, 2, sizes[0][0], TILE), bf16),
            tile,
            tile,
            *work(sizes[0][0], 2 * WIDE),
            *work(sizes[2][0], D // 2),
        ],
        compiler_params=pltpu.CompilerParams(collective_id=0, has_side_effects=True, vmem_limit_bytes=VMEM_LIMIT),
        name="backward",
    )(*args)


def solution(mesh):
    def step(x, dy, *arrays):
        weights, m, v = (arrays[i : i + 3] for i in (0, 3, 6))
        x, dy = x[0], dy[0]
        sizes = [t.shape[1:] for t in m]
        a0, act0, h1, a1 = forward(x, *weights)
        out = backward(sizes, a0, act0, h1, a1, dy, weights, m, v)
        return tuple(w.reshape(t.shape) for w, t in zip(out[:3], weights, strict=True)) + tuple(out[3:9])

    whole, rows, seq = P(None, None, None), P(None, "dp", None), P(("rep", "dp"), None, None)
    return jax.shard_map(
        step,
        mesh=mesh,
        in_specs=(seq, seq) + (whole,) * 3 + (rows,) * 6,
        out_specs=(P("rep", None, None),) * 3 + (P("rep", "dp", None),) * 6,
        check_vma=False,
    )
```

time: 1800 us -> 781 us (0.43)
  waiting for transfers between devices: 1100 us -> 0 us
  Pallas kernels: 0 us -> 720 us
  matrix products: 533 us -> 0 us
  other arithmetic: 78.2 us -> 0.01 us
    pallas_call x0 -> x3, Pallas kernels: none -> 720 us  [the longest x1 639 us: backward(): pl.pallas_call(functools.partial(backward_kernel, sizes), out_shape=outs,...]
    reduce_scatter x6 -> x0, waiting for transfers between devices: 615 us -> none  [step(): lax.psum_scatter(grads[number][name], 'dp', scatter_dimension=0, tiled=True)]
    dot_general x15 -> x0, matrix products: 533 us -> none  [the longest x5 190 us: layer(): gate = jnp.dot(a, w['w_gate'], preferred_element_type=jnp.float32)]
    all_gather x6 -> x0, waiting for transfers between devices: 480 us -> none  [step(): new[name][number] = (lax.all_gather(w, 'dp', axis=0, tiled=True), nm, nv)]
    another operation x6 -> x0, other arithmetic: 58.1 us -> none  [step(): jnp.stack([new[name][number][which] for number in range(layers)])]
    slice x3 -> x0, local copies, waits for them, and re-layouts: 48.7 us -> none  [the longest x2 32.3 us: step(): w[number]]
    unnamed x26 -> x33, local copies, waits for them, and re-layouts: 15.5 us -> 52.2 us
  transfers between devices with their start and end apart: 12 -> 0, of which waited for: 11 -> 0; matrix products, arithmetic and copies ran while one was open for 21% -> 0% of each run, Pallas kernels for 0% -> 0%
where the time goes in v3:
time: 781 us; the launch traced here: 773 us
  Pallas kernels  720 us (92%)
  local copies, waits for them, and re-layouts  52.2 us (7%)
    pallas_call x1, Pallas kernels, backward(): pl.pallas_call(functools.partial(backward_kernel, sizes), out_shape=outs,...  639 us
    unnamed x33, local copies, waits for them, and re-layouts  52.2 us
    pallas_call x1, Pallas kernels, forward(): pl.pallas_call(up_kernel, grid=(F // 512,), in_specs=[full, columns, colu...  51.6 us
    pallas_call x1, Pallas kernels, forward(): pl.pallas_call(down_kernel, grid=(T // 256,), in_specs=[row, pl.BlockSpec...  29.8 us

profile of v3, /device:TPU:0, one launch (start us, length us, event | category | flops | bytes accessed | tf_op | source)
XLA Modules:
  0.0 773.2 jit_solution(7505372731461837369)
XLA Ops:
  0.6 51.6 %up.1 = (bf16[2048,1024]{1,0:T(8,128)(2,1)}, bf16[2048,5120]{1,0:T(8,128)(2,1)}) custom-call(bf16[2048,1024]{1,0:T(8,128)(2,1)} %bitcast.16, bf16[2,1024,5120]{2,1,0:T(8,128)(2,1)} %refs_5_.1, bf16[2,1024,5120]{2,1,0:T(8,128)(2,1)} %refs_6_.1), custom_call_target="tpu_custom_call" | custom-call | tf_op jit(solution)/shard_map/up/pallas_call | solution.py:71
  52.3 29.8 %down.1 = (bf16[2048,1024]{1,0:T(8,128)(2,1)}, bf16[2048,1024]{1,0:T(8,128)(2,1)}) custom-call(bf16[2048,1024]{1,0:T(8,128)(2,1)} %bitcast.17, bf16[2048,5120]{1,0:T(8,128)(2,1)} %get-tuple-element.23.act.refs_1_, bf16[2,5120,1024]{2,1,0:T(8,128)(2,1)} %refs_7_.1), custom_call_target="tpu_custom_call" | custom-call | tf_op jit(solution)/shard_map/down/pallas_call | solution.py:83
  82.1 638.8 %backward.1 = (bf16[2,2,2,4,2,32,5120]{6,5,4,3,2,1,0:T(8,128)(2,1)}, bf16[2,2,2,4,2,32,5120]{6,5,4,3,2,1,0:T(8,128)(2,1)}, bf16[2,2,2,4,2,160,1024]{6,5,4,3,2,1,...) custom-call(bf16[2048,1024]{1,0:T(8,128)(2,1)} %get-tuple-element.22, ...), custom_call_target="tpu_custom_call" | custom-call | tf_op jit(solution)/shard_map/backward/pallas_call | solution.py:575
  720.9 0.0 copy-start
  720.9 0.0 slice-start
  720.9 0.0 slice-start.1
  721.0 0.0 slice-start.2
  721.0 21.0 %copy.29 = bf16[2,1024,5120]{2,1,0:T(8,128)(2,1)} copy(bf16[2,1024,5120]{2,1,0:T(8,128)(2,1)} %bitcast.15) | data formatting | bytes 41943040
  741.9 0.0 copy-done
  741.9 0.0 slice-start.3
  741.9 0.0 slice-start.4
  741.9 10.6 %copy.30 = bf16[2,1024,5120]{2,1,0:T(8,128)(2,1)} copy(bf16[2,1024,5120]{2,1,0:T(8,128)(2,1)S(1)} %bitcast.14) | data formatting | bytes 41943040
  752.6 0.0 slice-done
  752.6 0.0 slice-done.1
  752.6 0.0 slice-done.2
  752.6 1.9 slice-done.3
  754.4 1.2 slice-done.4
  755.6 0.0 copy-start.6
  755.6 7.5 copy.31
  763.2 0.0 copy-done.6
  763.2 0.0 copy-start.5
  763.2 1.1 copy.32
  764.2 0.7 copy-done.5
  765.0 0.0 copy-start.4
  765.0 1.1 copy.33
  766.0 0.7 copy-done.4
  766.8 0.0 copy-start.3
  766.8 1.1 copy.34
  767.8 0.7 copy-done.3
  768.5 0.0 copy-start.2
  768.5 1.1 copy.35
  769.6 0.7 copy-done.2
  770.3 0.0 copy-start.1
  770.3 1.1 copy.36
  771.4 0.7 copy-done.1
  772.1 1.1 copy.37
  (1 shorter events, 0.0 us)
Async XLA Ops:
  720.9 21.0 %copy-start = (bf16[2,2,2,4,2,32,5120]{6,5,4,3,2,1,0:T(8,128)(2,1)S(1)}, bf16[2,2,2,4,2,32,5120]{6,5,4,3,2,1,0:T(8,128)(2,1)}, u32[]{:S(2)}) copy-start(bf16[2,2,2,4,2,32,5120]{6,5,4,3,2,1,0:T(8,128)(2,1)} %get-tuple-element.27) | copy-start | bytes 62914564
  720.9 31.6 %slice-start = ((s8[20971520]{0:T(1024)(128)(4,1)}), s8[4194304]{0:T(1024)(128)(4,1)S(1)}, s32[]{:S(2)}) async-start(s8[20971520]{0:T(1024)(128)(4,1)} %bitcast.11), calls=%async_computation | async-start | bytes 8388608
  720.9 31.6 %slice-start.1 = ((s8[20971520]{0:T(1024)(128)(4,1)}), s8[4194304]{0:T(1024)(128)(4,1)S(1)}, s32[]{:S(2)}) async-start(s8[20971520]{0:T(1024)(128)(4,1)} %bitcast.11), calls=%async_computation.1 | async-start | bytes 8388608
  721.0 31.6 %slice-start.2 = ((s8[20971520]{0:T(1024)(128)(4,1)}), s8[4194304]{0:T(1024)(128)(4,1)S(1)}, s32[]{:S(2)}) async-start(s8[20971520]{0:T(1024)(128)(4,1)} %bitcast.11), calls=%async_computation.2 | async-start | bytes 8388608
  741.9 12.5 %slice-start.3 = ((s8[20971520]{0:T(1024)(128)(4,1)}), s8[4194304]{0:T(1024)(128)(4,1)S(1)}, s32[]{:S(2)}) async-start(s8[20971520]{0:T(1024)(128)(4,1)} %bitcast.11), calls=%async_computation.3 | async-start | bytes 8388608
  741.9 13.7 %slice-start.4 = ((s8[20971520]{0:T(1024)(128)(4,1)}), s8[4194304]{0:T(1024)(128)(4,1)S(1)}, s32[]{:S(2)}) async-start(s8[20971520]{0:T(1024)(128)(4,1)} %bitcast.11), calls=%async_computation.4 | async-start | bytes 8388608
  755.6 7.5 copy-start.6
  763.2 1.8 copy-start.5
  765.0 1.8 copy-start.4
  766.8 1.8 copy-start.3
  768.5 1.8 copy-start.2
  770.3 1.8 copy-start.1

commit v4 on v1

v4 whole, which is shorter than its diff:
```python
import functools

import jax
import jax.numpy as jnp
from jax import lax
from jax.experimental import pallas as pl
from jax.experimental.pallas import tpu as pltpu
from jax.sharding import PartitionSpec as P

MESH = pl.DeviceIdType.MESH
f32, bf16 = jnp.float32, jnp.bfloat16
T, D, F, LAYERS = 2048, 1024, 5120, 2
TILE = 256
STEPS = F // TILE
CHIPS = (2, 2, 4)
N = None
EVERY = slice(None)
VMEM_LIMIT = 63 << 20
NT = (((1,), (1,)), ((), ()))
TN = (((0,), (0,)), ((), ()))


def dot(a, b):
    return jnp.dot(a, b, preferred_element_type=f32)


def dot_nt(a, b):
    return lax.dot_general(a, b, NT, preferred_element_type=f32)


def dot_tn(a, b):
    return lax.dot_general(a, b, TN, preferred_element_type=f32)


def normed(h):
    wide = h.astype(f32)
    scale = lax.rsqrt(jnp.mean(wide**2, -1, keepdims=True) + 1e-6)
    return (wide * scale).astype(bf16)


def forward(layer, x_in, wg, wu, wd, act, a, acc, h_scr, a_scr, sem):
    a_out = pltpu.make_async_copy(a_scr, a, sem)

    def body(step, wg, wu, wd, act):
        @pl.when(step.index[0] == 0)
        def _():
            x_in.wait()

            @pl.loop(0, T // 256)
            def _(m):
                s = pl.ds(m * 256, 256)
                a_scr[s, :] = normed(h_scr[s, :])
                acc[s, :] = jnp.zeros((256, D), f32)

            a_out.start()

        def rows(m, _):
            s = pl.ds(m * 512, 512)
            gate, up = dot(a_scr[s, :], wg[...]), dot(a_scr[s, :], wu[...])
            product = (gate * (1.0 / (1.0 + jnp.exp(-gate))) * up).astype(bf16)
            act[s, :] = product
            acc[s, :] += dot(product, wd[...])
            return 0

        lax.fori_loop(0, T // 512, rows, 0, unroll=4)

    columns = pl.BlockSpec((N, D, 512), lambda j: (layer, 0, j))
    pltpu.emit_pipeline(
        body,
        grid=(F // 512,),
        in_specs=[columns, columns, pl.BlockSpec((N, 512, D), lambda j: (layer, j, 0))],
        out_specs=[pl.BlockSpec((T, 512), lambda j: (0, j))],
        _explicit_indices=True,
    )(wg, wu, wd, act)
    a_out.wait()

    @pl.loop(0, T // 256)
    def _(m):
        s = pl.ds(m * 256, 256)
        h = h_scr[s, :] + acc[s, :].astype(bf16)
        h_scr[s, :] = h
        a_scr[s, :] = normed(h)


def index(x, y, z, c):
    return ((x * 2 + y) * 4 + z) * 2 + c


class Me:
    def __init__(self):
        d = lax.axis_index("dp")
        self.c = lax.rem(d, 2)
        self.z = lax.rem(lax.div(d, 2), 4)
        self.y = lax.rem(lax.div(d, 8), 2)
        self.x = lax.div(d, 16)
        self.inner = jnp.logical_and(self.z != 0, self.z != 3)
        self.core = index(self.x, self.y, self.z, 1 - self.c)
        self.xn = index(1 - self.x, self.y, self.z, self.c)
        self.yn = index(self.x, 1 - self.y, self.z, self.c)
        self.zn = {k: index(self.x, self.y, lax.rem(self.z + k, 4), self.c) for k in (1, 2, 3)}


def barrier(me):
    sem = pltpu.get_barrier_semaphore()
    peers = [me.core, me.xn, me.yn, *me.zn.values()]
    for peer in peers:
        pl.semaphore_signal(sem, inc=1, device_id=(0, peer), device_id_type=MESH)
    return functools.partial(pl.semaphore_wait, sem, len(peers))


def pick(k, a, b):
    return (1 - k) * a + k * b


KEYS = ("core", "xy1", "xy2", "z", "a1", "a2", "a21", "a22", "a23", "relay", "a3", "ac1", "ac2", "ac3")


class Piece:
    def __init__(self, me, sems, layer, r, C, G, first, bufs, parts, z_late, tmp):
        self.me, self.l, self.r, self.C, self.parts, self.z_late, self.tmp = me, layer, r, C, parts, z_late, tmp
        self.G, self.cols = G, pl.ds(first, C)
        self.R0, self.S0, self.R1, self.S1, self.R2, self.S2, self.R3 = bufs
        self.sems = {key: sems.take() for key in KEYS}
        sums = zip((self.s1, self.s2, self.s3, self.s4), ("core", "xy1", "xy2", "z"), strict=True)
        stages = [functools.partial(self.part, stage, key, i) for stage, key in sums for i in range(3)]
        self.stages = iter([self.s0, *stages, self.g1, *([self.g2] if z_late else []), self.g3, self.g4])

    def part(self, stage, key, i):
        if not i:
            self.wait(key)
        stage()[i]()

    def g(self, *spot):
        return self.G.at[(*spot, self.cols)]

    def pairs(self, key):
        me, h = self.me, self.r // 2
        x, y, z, c = me.x, me.y, me.z, me.c
        if key == "core":
            return [(self.g(EVERY, EVERY, EVERY, 1 - c, EVERY), self.R0, me.core)]
        if key == "xy1":
            return [(self.S0.at[0], self.R1.at[0], me.xn), (self.S0.at[1], self.R1.at[1], me.yn)]
        if key == "xy2":
            return [(self.S1.at[0], self.R2.at[0], me.yn), (self.S1.at[1], self.R2.at[1], me.xn)]
        if key == "z":
            return [(self.S2.at[lax.rem(z + k, 4)], self.R3.at[k - 1], me.zn[k]) for k in (1, 2, 3)]
        out = []
        for part in self.parts:
            cols = pl.ds(part["first"], part["width"])
            lo, hi = pl.ds(0, h), pl.ds(h, h)

            def w(a, b, d, rows):
                return part["W"].at[self.l, a, b, d, c, rows, cols]

            if key == "a1" and not self.z_late:
                spots = [(w(x, y, z, EVERY), me.zn[k]) for k in (1, 2, 3)]
            elif key == "a2":
                spots = [(w(x, y, EVERY, lo), me.yn), (w(x, y, EVERY, hi), me.xn)]
            elif key == "ac1":
                spots = [(w(x, y, EVERY, EVERY), me.core)]
            elif key == "ac2" and not self.z_late:
                spots = [(w(x, 1 - y, EVERY, lo), me.core), (w(1 - x, y, EVERY, hi), me.core)]
            elif key == "a1":
                spots = [(w(x, y, z, lo), me.yn), (w(x, y, z, hi), me.xn)]
            elif key[:2] == "a2":
                k = int(key[2])
                spots = [(w(x, EVERY, z, lo), me.zn[k]), (w(EVERY, y, z, hi), me.zn[k])]
            elif key == "relay":
                far, near = pick(z - 1, 3, 0), pick(z - 1, 0, 3)
                to = index(x, y, near, c)
                spots = [(w(x, EVERY, far, lo), to), (w(EVERY, y, far, hi), to)]
            elif key == "a3":
                spots = [(w(x, EVERY, EVERY, lo), me.xn), (w(EVERY, y, EVERY, hi), me.yn)]
            elif key == "ac2":
                spots = [(w(x, EVERY, EVERY, lo), me.core), (w(EVERY, y, EVERY, hi), me.core)]
            else:
                spots = [(w(1 - x, EVERY, EVERY, lo), me.core), (w(EVERY, 1 - y, EVERY, hi), me.core)]
            out += [(ref, ref, dev) for ref, dev in spots]
        return out

    def start(self, *keys):
        for key in keys:
            send, recv = self.sems[key]
            for src, dst, dev in self.pairs(key):
                pltpu.make_async_remote_copy(src_ref=src, dst_ref=dst, send_sem=send, recv_sem=recv, device_id=(0, dev), device_id_type=MESH).start()

    def whole(self, key):
        sizes = {"core": self.R0, "z": self.R3, "a1": self.R3.at[0], "xy1": self.R1, "xy2": self.R2, "ac2": self.R0.at[0]}
        if not self.z_late:
            sizes |= {"a1": self.R3, "a2": self.R2, "ac1": self.R2, "ac2": self.R2}
        if key in sizes:
            return sizes[key]
        return self.R3.at[pl.ds(0, 2)] if key[:2] in ("a2", "re") else self.R1

    def wait(self, *keys, which=1):
        for key in keys:
            pltpu.make_async_copy(self.whole(key), self.whole(key), self.sems[key][which]).wait()

    def half(self, k):
        return pl.ds(k * (self.r // 2), self.r // 2)

    def add(self, terms, outs, key):
        V, sem = self.tmp["V"], self.tmp["sem"]
        n, flat = len(terms[0]), len(terms[0][0].shape) == 3
        a, b = (1, terms[0][0].shape[0]) if flat else terms[0][0].shape[:2]
        cols = EVERY if self.C == V.shape[-1] else pl.ds(0, self.C)

        def spot(i):
            return (i // 2, i % 2) if flat else (i, EVERY)

        def view(i, k):
            return V.at[spot(i)[0], k, spot(i)[1], :, :, cols]

        out = 5 if flat else 2

        def stores():
            return [pltpu.make_async_copy(view(out, k), outs[k], sem.at[2 + k]) for k in range(2)]

        def load():
            for k in range(2):
                for i, term in enumerate(terms[k]):
                    pltpu.make_async_copy(term, view(i, k), sem.at[k]).start()

        def compute():
            for k in range(2):
                all_of = V.at[pl.ds(0, 3), k, 0, :, :, cols] if n == 3 else V.at[pl.ds(0, 2), k, :, :, :, cols]
                pltpu.make_async_copy(all_of, all_of, sem.at[k]).wait()

                @pl.loop(0, a * b)
                def _(j):
                    q, d = j // b, lax.rem(j, b)

                    def block(i):
                        return (i // 2, k, i % 2, j, EVERY, cols) if flat else (i, k, q, d, EVERY, cols)

                    total = V[block(0)].astype(f32)
                    for i in range(1, n):
                        total = total + V[block(i)].astype(f32)
                    V[block(out)] = total.astype(bf16)

                stores()[k].start()

        def send():
            for store in stores():
                store.wait()
            self.start(key)

        return load, compute, send

    def s0(self):
        self.start("core")

    def s1(self):
        me = self.me
        G, R0, lo, hi = self.g, self.R0, self.half(0), self.half(1)
        return self.add(
            [
                [G(1 - me.x, EVERY, EVERY, me.c, lo), R0.at[1 - me.x, :, :, lo]],
                [G(EVERY, 1 - me.y, EVERY, me.c, hi), R0.at[:, 1 - me.y, :, hi]],
            ],
            [self.S0.at[0], self.S0.at[1]],
            "xy1",
        )

    def s2(self):
        me = self.me
        G, R0, R1, lo, hi = self.g, self.R0, self.R1, self.half(0), self.half(1)
        return self.add(
            [
                [G(me.x, 1 - me.y, EVERY, me.c, lo), R0.at[me.x, 1 - me.y, :, lo], R1.at[0, 1 - me.y]],
                [G(1 - me.x, me.y, EVERY, me.c, hi), R0.at[1 - me.x, me.y, :, hi], R1.at[1, 1 - me.x]],
            ],
            [self.S1.at[0], self.S1.at[1]],
            "xy2",
        )

    def s3(self):
        me = self.me
        x, y = me.x, me.y
        return self.add(
            [
                [self.g(x, y, EVERY, me.c, self.half(k)), self.R0.at[x, y, :, self.half(k)], self.R1.at[k, (y, x)[k]], self.R2.at[k]]
                for k in range(2)
            ],
            [self.S2.at[:, self.half(0)], self.S2.at[:, self.half(1)]],
            "z",
        )

    def s4(self):
        me, l, h = self.me, self.l, self.r // 2
        x, y, z, c = me.x, me.y, me.z, me.c
        BB, AA, sem = self.tmp["B"], self.tmp["A"], self.tmp["sem"]
        width = self.C // len(self.parts)
        lo, hi = self.half(0), self.half(1)
        whole = self.C == BB.shape[-1]

        class At:
            def __init__(self, ref, C):
                self.ref, self.cols = ref, EVERY if whole else pl.ds(0, C)

            def at(self, *spot):
                spot += (EVERY,) * (2 - len(spot))
                return self.ref.at[spot if len(spot) == 3 else (*spot, self.cols)]

        B, A = At(BB, self.C).at, At(AA, self.C).at
        terms = [(self.g(x, y, z, c, EVERY), B(0)), (self.R0.at[x, y, z], B(1)), (self.R3, B(pl.ds(4, 3)))]
        terms += [(self.R1.at[0, y, z], B(2, lo)), (self.R1.at[1, x, z], B(2, hi))]
        terms += [(self.R2.at[0, z], B(3, lo)), (self.R2.at[1, z], B(3, hi))]
        moments, w_out, out = [], [], []
        for p, part in enumerate(self.parts):
            there, here = pl.ds(part["first"], width), pl.ds(p * width, width)
            terms += [(part["w"].at[l, x, y, z, c, :, there], B(7, EVERY, here))]
            moments += [(part["m"].at[l, :, there], A(0, EVERY, here)), (part["v"].at[l, :, there], A(1, EVERY, here))]
            w_out += [(B(8, EVERY, here), part["W"].at[l, x, y, z, c, :, there])]
            out += [(B(0, EVERY, here), part["g"].at[l, :, there])]

        def begin(pairs, i):
            for src, dst in pairs:
                pltpu.make_async_copy(src, dst, sem.at[i]).start()

        def end(ref, i):
            pltpu.make_async_copy(ref, ref, sem.at[i]).wait()

        def load():
            begin(terms, 4)
            begin(moments, 5)

        def compute():
            end(B(pl.ds(0, 8)), 4)
            end(A(pl.ds(0, 2)), 5)
            blocks, across = self.r // 16, self.C // 512

            @pl.loop(0, blocks * across)
            def _(j):
                rows = pl.ds(pl.multiple_of(lax.rem(j, blocks) * 16, 16), 16)
                cols = pl.ds(pl.multiple_of(j // blocks * 512, 512), 512)
                t = BB[0, rows, cols].astype(f32)
                for i in range(1, 7):
                    t = t + BB[i, rows, cols].astype(f32)
                t = t.astype(bf16)
                BB[0, rows, cols] = t
                t = t.astype(f32)
                m = 0.9 * AA[0, rows, cols] + 0.1 * t
                v = 0.95 * AA[1, rows, cols] + 0.05 * t * t
                w = BB[7, rows, cols].astype(f32)
                BB[8, rows, cols] = (w - 0.02 * (m * lax.rsqrt(v + 1e-8) + 0.1 * w)).astype(bf16)

            begin(w_out, 6)
            begin(out, 7)

        def send():
            end(B(8), 6)
            end(B(0), 7)
            self.start("a1")

        return load, compute, send

    def g1(self):
        self.wait("a1")
        if not self.z_late:
            self.start("a2", "ac1")
            return
        self.start("a22")
        pl.when(self.me.z != 3)(lambda: self.start("a21"))
        pl.when(self.me.z != 0)(lambda: self.start("a23"))

    def g2(self):
        self.wait("a22")
        pl.when(self.me.z != 0)(lambda: self.wait("a21"))
        pl.when(self.me.z != 3)(lambda: self.wait("a23"))
        pl.when(self.me.inner)(lambda: self.start("relay"))

    def g3(self):
        if self.z_late:
            pl.when(jnp.logical_not(self.me.inner))(lambda: self.wait("relay"))
        else:
            self.wait("a2")
        self.start("a3", "ac2")

    def g4(self):
        self.wait("a3")
        self.start("ac3")

    def end(self):
        self.wait("core", "xy1", "xy2", "z", "a1", "a3", "ac2", "ac3", which=0)
        self.wait("ac2", "ac3")
        if self.z_late:
            self.wait("a22", which=0)
            pl.when(self.me.z != 3)(lambda: self.wait("a21", which=0))
            pl.when(self.me.z != 0)(lambda: self.wait("a23", which=0))
            pl.when(self.me.inner)(lambda: self.wait("relay", which=0))
        else:
            self.wait("ac1")
            self.wait("a2", "ac1", which=0)


class Sems:
    def __init__(self, send=None, recv=None):
        self.send, self.recv, self.n = send, recv, 0

    def take(self):
        self.n += 1
        return self.send.at[self.n - 1], self.recv.at[self.n - 1]


def buffers(r, C):
    h = r // 2
    quarter, eighth = (*CHIPS, h, C), (*CHIPS[1:], h, C)
    shapes = (*CHIPS, r, C), quarter, quarter, eighth, eighth, (4, r, C), (3, r, C)
    return [jax.ShapeDtypeStruct(s, bf16) for s in shapes]


WIDE_1 = (2, 4, 4, 5, 5)
WIDE_0 = (5, 5, 5, 3, 2)
Z_LATE = "-----zz-z--zzz"
PLAN = (
    ("----a--a-a-a---a-ab-a-b-b-ba-a-a--c-ab-ab-abc-cc-ab-b-b--c-c", "dac-b-bd-bda-dc-cc--b--d",),
    ("bdec-dcc--e-be-e-cd-d",),
    ("gfde-ec-eg-ggfd-fdcf-de-e-e-g-gdg",),
    ("def-effeg-gg---d-e",),
    ("eifh-gffgg-i-i-eih-ghhf-ff---i-ji-i-g-jh-jhfhj-gi-i-ih-hh--k", "-fj-j-jk-kfk-gi-i-ij-j-hj-lhh-f-l-ll-j-kjkijk-m-h-mmml-ll",),
)
TAIL = ("nkkknnhinmimmjlllkhkknnnlllimmkmjnnlnmmmkjmlnnnlknmmnlnmn",)
COUNT = len(WIDE_1) + len(WIDE_0) + 4


def starts(sizes):
    return [sum(sizes[:q]) for q in range(len(sizes))]


def hidden_backward(layer, sizes, wg, wu, wd, keep, G, a_scr, dh_scr, gbuf, gsem, scratch, hook):
    def out_copies(i):
        first = size = 0
        for start, n in zip(starts(sizes), sizes, strict=True):
            first, size = jnp.where(i >= start, start, first), jnp.where(i >= start, n, size)
        return [
            pltpu.make_async_copy(gbuf.at[k], G.at[:, :, :, :, :, pl.ds(pl.multiple_of((i + first + k * size) * TILE, TILE), TILE)], gsem.at[k])
            for k in range(2)
        ]

    def body(step, wg, wu, wd, *outs):
        i = step.index[0]
        act, dg, du = outs if keep else (None, *scratch)

        def rows(m, _):
            s = pl.ds(m * 512, 512)
            a = a_scr[s, :]
            gate, up, d = dot(a, wg[...]), dot(a, wu[...]), dot_nt(dh_scr[s, :], wd[...])
            d = d.astype(bf16).astype(f32)
            sig = 1.0 / (1.0 + jnp.exp(-gate))
            silu = gate * sig
            if keep:
                act[s, :] = (silu * up).astype(bf16)
            du[s, :] = (d * silu).astype(bf16)
            dg[s, :] = (d * up * (sig + silu * (1.0 - sig))).astype(bf16)
            return 0

        lax.fori_loop(0, T // 512, rows, 0, unroll=4)

        @pl.when(i > 0)
        def _():
            for copy in out_copies(i - 1):
                copy.wait()

        hook(i, 0, 2)
        gbuf[0] = dot_tn(a_scr[...], dg[...]).astype(bf16).reshape(gbuf.shape[1:])
        gbuf[1] = dot_tn(a_scr[...], du[...]).astype(bf16).reshape(gbuf.shape[1:])
        for copy in out_copies(i):
            copy.start()
        hook(i, 1, 2)

    columns = pl.BlockSpec((N, D, TILE), lambda i: (layer, 0, i))
    tile = pl.BlockSpec((T, TILE), lambda i: (0, i))
    pltpu.emit_pipeline(
        body,
        grid=(STEPS,),
        in_specs=[columns, columns, pl.BlockSpec((N, TILE, D), lambda i: (layer, i, 0))],
        out_specs=[tile] * 3 if keep else [],
        _explicit_indices=True,
    )(wg, wu, wd, *(keep or ()))
    for copy in out_copies(STEPS - 1):
        copy.wait()


def down_gradient(act, G, dh_scr, hook):
    def body(step, act, g):
        @pl.loop(0, 2)
        def _(k):
            cols = pl.ds(pl.multiple_of(k * (D // 2), D // 2), D // 2)
            g[k] = dot_tn(act[...], dh_scr[:, cols]).astype(bf16).reshape(g.shape[1:])

        hook(step.index[0])

    out = pl.BlockSpec((2, N, N, 2, 2, 160, D // 2), lambda i: (0, i // 4, lax.rem(i // 2, 2), lax.rem(i, 2), 0, 0, 0))
    pltpu.emit_pipeline(
        body, grid=(8,), in_specs=[pl.BlockSpec((T, 640), lambda i: (0, i))], out_specs=[out], _explicit_indices=True
    )(act, G)


def state_gradient(layer, dg, du, wg, wu, acc, hook):
    def body(step, dg, du, wg, wu):
        i = step.index[0]

        @pl.when(i == 0)
        def _():
            acc[...] = jnp.zeros_like(acc)

        @pl.loop(0, 2)
        def _(m):
            s = pl.ds(m * (T // 2), T // 2)
            acc[s, :] += dot_nt(dg[s, :], wg[...]) + dot_nt(du[s, :], wu[...])

        hook(i)

    tile = pl.BlockSpec((T, 512), lambda i: (0, i))
    columns = pl.BlockSpec((N, D, 512), lambda i: (layer, 0, i))
    pltpu.emit_pipeline(body, grid=(F // 512,), in_specs=[tile, tile, columns, columns], _explicit_indices=True)(dg, du, wg, wu)


def through_norm(acc, h_scr, dh_scr):
    @pl.loop(0, T // 256)
    def _(m):
        s = pl.ds(m * 256, 256)
        da = acc[s, :].astype(bf16).astype(f32)
        wide = h_scr[s, :].astype(f32)
        scale = lax.rsqrt(jnp.mean(wide**2, -1, keepdims=True) + 1e-6)
        along = jnp.sum(da * wide, -1, keepdims=True) * (1.0 / D)
        d = da * scale - wide * (scale * scale * scale * along)
        dh_scr[s, :] = dh_scr[s, :] + d.astype(bf16)


def step_kernel(sizes, *refs):
    (x, dy), w3, w7, m, v, refs = refs[:2], refs[2:5], refs[5:8], refs[8:11], refs[11:14], refs[14:]
    W, g, (a0, act0, act, dg, du), Gs, refs = refs[:3], refs[3:6], refs[6:11], refs[11:15], refs[15:]
    bufs, refs = refs[: 7 * COUNT], refs[7 * COUNT :]
    send, recv, load_sem, gsem, work_sem, a_scr, h_scr, dh_scr, acc, gbuf, dg_scr, du_scr, V_wide, B_wide, A_wide, V_down, B_down, A_down = refs
    G1, G1d, G0d, G0 = Gs
    me = Me()
    arrived = barrier(me)
    sems = Sems(send, recv)

    def part(i, first, width):
        return dict(w=w7[i], m=m[i], v=v[i], W=W[i], g=g[i], first=first, width=width)

    def piece(layer, r, C, G, first, parts, V, B, A):
        u = len(pieces)
        work = dict(V=V, B=B, A=A, sem=work_sem.at[pl.ds(0 if V is V_wide else 8, 8)])
        pieces.append(Piece(me, sems, layer, r, C, G, first, bufs[7 * u : 7 * u + 7], parts, Z_LATE[u] == "z", work))

    def wide_pieces(layer, tiles, G):
        for start, n in zip(starts(tiles), tiles, strict=True):
            parts = [part(i, start * TILE, n * TILE) for i in range(2)]
            piece(layer, sizes[0][0], 2 * n * TILE, G, 2 * start * TILE, parts, V_wide, B_wide, A_wide)

    def down_pieces(layer, G):
        for q in range(2):
            piece(layer, sizes[2][0], D // 2, G.at[q], 0, [part(2, q * (D // 2), D // 2)], V_down, B_down, A_down)

    pieces = []
    wide_pieces(1, WIDE_1, G1)
    down_pieces(1, G1d)
    down_pieces(0, G0d)
    wide_pieces(0, WIDE_0, G0)

    plan = [
        [[next(pieces[ord(letter) - ord("a")].stages) for letter in letters] for letters in "".join(host).split("-")]
        for host in (*PLAN, TAIL)
    ]

    def run(stages):
        for stage in stages:
            stage()

    def hook_of(host):
        def among(i, jobs):
            if len(jobs) > 1:
                middle = jobs[len(jobs) // 2][0]
                pl.when(i < middle)(lambda: among(i, jobs[: len(jobs) // 2]))
                pl.when(i >= middle)(lambda: among(i, jobs[len(jobs) // 2 :]))
            elif jobs:
                pl.when(i == jobs[0][0])(lambda: run(jobs[0][1]))

        def hook(i, place=0, places=1):
            among(i, [job for job in enumerate(plan[host][place::places]) if job[1]])

        return hook

    x_in = pltpu.make_async_copy(x, h_scr, load_sem.at[0])
    dy_in = pltpu.make_async_copy(dy, dh_scr, load_sem.at[1])
    x_in.start()
    dy_in.start()
    forward(0, x_in, *w3, act0, a0, acc, h_scr, a_scr, load_sem.at[2])
    dy_in.wait()
    arrived()
    hidden_backward(1, WIDE_1, *w3, (act, dg, du), G1, a_scr, dh_scr, gbuf, gsem, None, hook_of(0))
    a0_in = pltpu.make_async_copy(a0, a_scr, load_sem.at[0])
    a0_in.start()
    down_gradient(act, G1d, dh_scr, hook_of(1))
    state_gradient(1, dg, du, w3[0], w3[1], acc, hook_of(2))
    through_norm(acc, h_scr, dh_scr)
    a0_in.wait()
    down_gradient(act0, G0d, dh_scr, hook_of(3))
    hidden_backward(0, WIDE_0, *w3, None, G0, a_scr, dh_scr, gbuf, gsem, (dg_scr, du_scr), hook_of(4))
    run(*plan[-1])
    for one in pieces:
        one.end()


def run_step(sizes, x, dy, weights, m, v):
    hbm = pl.BlockSpec(memory_space=pl.ANY)

    def shape(s, dtype=bf16):
        return jax.ShapeDtypeStruct(s, dtype)

    views = [w.reshape(LAYERS, *CHIPS, 2, *s) for w, s in zip(weights, sizes, strict=True)]
    args = [x, dy, *weights, *views, *m, *v]
    outs = [shape(w.shape) for w in views] + [shape((LAYERS, *s)) for s in sizes] + [shape((T, D))] + [shape((T, F))] * 4
    wide, down = shape((*CHIPS, 2, sizes[0][0], 2 * F)), shape((2, *CHIPS, 2, sizes[2][0], D // 2))
    outs += [wide, down, down, wide]
    for n in (*WIDE_1, 0, 0, 0, 0, *WIDE_0):
        outs += buffers(sizes[0][0], 2 * n * TILE) if n else buffers(sizes[2][0], D // 2)
    count = COUNT * len(KEYS)
    tokens = pltpu.VMEM((T, D), bf16)
    tile = pltpu.VMEM((T, TILE), bf16)

    def work(r, C):
        return pltpu.VMEM((3, *CHIPS, r // 2, C), bf16), pltpu.VMEM((9, r, C), bf16), pltpu.VMEM((2, r, C), f32)

    return pl.pallas_call(
        functools.partial(step_kernel, sizes),
        out_shape=outs,
        in_specs=[hbm] * len(args),
        out_specs=[hbm] * len(outs),
        scratch_shapes=[
            pltpu.SemaphoreType.DMA((count,)),
            pltpu.SemaphoreType.DMA((count,)),
            pltpu.SemaphoreType.DMA((3,)),
            pltpu.SemaphoreType.DMA((2,)),
            pltpu.SemaphoreType.DMA((16,)),
            tokens,
            tokens,
            tokens,
            pltpu.VMEM((T, D), f32),
            pltpu.VMEM((2, *CHIPS, 2, sizes[0][0], TILE), bf16),
            tile,
            tile,
            *work(sizes[0][0], 2 * max(WIDE_1 + WIDE_0) * TILE),
            *work(sizes[2][0], D // 2),
        ],
        compiler_params=pltpu.CompilerParams(collective_id=0, has_side_effects=True, vmem_limit_bytes=VMEM_LIMIT),
        name="step",
    )(*args)


def solution(mesh):
    def step(x, dy, *arrays):
        weights, m, v = (arrays[i : i + 3] for i in (0, 3, 6))
        x, dy = x[0], dy[0]
        sizes = [t.shape[1:] for t in m]
        out = run_step(sizes, x, dy, weights, m, v)
        g = [t.astype(f32) for t in out[3:6]]
        new_m = [0.9 * m + 0.1 * g for m, g in zip(m, g, strict=True)]
        new_v = [0.95 * v + 0.05 * g * g for v, g in zip(v, g, strict=True)]
        return (*(w.reshape(t.shape) for w, t in zip(out[:3], weights, strict=True)), *new_m, *new_v)

    whole, rows, seq = P(None, None, None), P(None, "dp", None), P(("rep", "dp"), None, None)
    return jax.shard_map(
        step,
        mesh=mesh,
        in_specs=(seq, seq) + (whole,) * 3 + (rows,) * 6,
        out_specs=(P("rep", None, None),) * 3 + (P("rep", "dp", None),) * 6,
        check_vma=False,
    )
```

time: 1800 us -> 702 us (0.39)
  waiting for transfers between devices: 1100 us -> 0 us
  Pallas kernels: 0 us -> 652 us
  matrix products: 533 us -> 0 us
  other arithmetic: 78.2 us -> 8.31 us
  local copies, waits for them, and re-layouts: 64.1 us -> 38.9 us
    pallas_call x0 -> x1, Pallas kernels: none -> 652 us  [run_step(): pl.pallas_call(functools.partial(step_kernel, sizes), out_shape=outs, in_...]
    reduce_scatter x6 -> x0, waiting for transfers between devices: 615 us -> none  [step(): lax.psum_scatter(grads[number][name], 'dp', scatter_dimension=0, tiled=True)]
    dot_general x15 -> x0, matrix products: 533 us -> none  [the longest x5 190 us: layer(): gate = jnp.dot(a, w['w_gate'], preferred_element_type=jnp.float32)]
    all_gather x6 -> x0, waiting for transfers between devices: 480 us -> none  [step(): new[name][number] = (lax.all_gather(w, 'dp', axis=0, tiled=True), nm, nv)]
    another operation x6 -> x0, other arithmetic: 58.1 us -> none  [step(): jnp.stack([new[name][number][which] for number in range(layers)])]
    slice x3 -> x0, local copies, waits for them, and re-layouts: 48.7 us -> none  [the longest x2 32.3 us: step(): w[number]]
    unnamed x26 -> x33, local copies, waits for them, and re-layouts: 15.5 us -> 38.9 us
  transfers between devices with their start and end apart: 12 -> 0, of which waited for: 11 -> 0; matrix products, arithmetic and copies ran while one was open for 21% -> 0% of each run, Pallas kernels for 0% -> 0%
where the time goes in v4:
time: 702 us; the launch traced here: 701 us
  Pallas kernels  652 us (93%)
  local copies, waits for them, and re-layouts  38.9 us (6%)
  other arithmetic  8.31 us (1%)
    pallas_call x1, Pallas kernels, run_step(): pl.pallas_call(functools.partial(step_kernel, sizes), out_shape=outs, in_...  652 us
    unnamed x33, local copies, waits for them, and re-layouts  38.9 us

profile of v4, /device:TPU:0, one launch (start us, length us, event | category | flops | bytes accessed | tf_op | source)
XLA Modules:
  0.0 700.5 jit_solution(7411097485477320152)
XLA Ops:
  0.6 652.5 %step.1 = (bf16[2,2,2,4,2,32,5120]{6,5,4,3,2,1,0:T(8,128)(2,1)}, bf16[2,2,2,4,2,32,5120]{6,5,4,3,2,1,0:T(8,128)(2,1)}, bf16[2,2,2,4,2,160,1024]{6,5,4,3,2,1,0:T(...) custom-call(bf16[2048,1024]{1,0:T(8,128)(2,1)} %bitcast.18, ...), custom_call_target="tpu_custom_call" | custom-call | tf_op jit(solution)/shard_map/step/pallas_call | solution.py:629
  653.1 0.0 copy-start
  653.1 0.0 copy-start.1
  653.2 0.0 copy-start.2
  653.2 0.0 copy-start.3
  653.2 0.0 copy-start.4
  653.2 4.2 fusion.5
  657.4 0.0 copy-done
  657.4 0.0 copy-done.1
  657.4 0.0 copy-done.2
  657.4 0.0 copy-done.3
  657.4 0.0 copy-done.4
  657.4 0.0 slice-start.5
  657.4 0.0 slice-start.6
  657.4 4.1 fusion.3
  661.6 0.0 slice-start.7
  661.6 0.0 slice-start.8
  661.6 0.0 slice-start.9
  661.6 0.0 slice-start
  661.6 0.0 slice-start.1
  661.6 0.0 slice-start.2
  661.6 21.2 %copy.23 = bf16[2,1024,5120]{2,1,0:T(8,128)(2,1)} copy(bf16[2,1024,5120]{2,1,0:T(8,128)(2,1)} %bitcast.17) | data formatting | bytes 41943040
  682.8 0.0 slice-done.5
  682.8 0.0 slice-done.6
  682.8 0.0 slice-done.7
  682.8 0.0 slice-done.8
  682.8 0.0 slice-done.9
  682.9 0.0 slice-start.3
  682.9 0.0 slice-start.4
  682.9 10.0 %copy.24 = bf16[2,1024,5120]{2,1,0:T(8,128)(2,1)} copy(bf16[2,1024,5120]{2,1,0:T(8,128)(2,1)S(1)} %bitcast.16) | data formatting | bytes 41943040
  692.9 0.0 slice-done
  692.9 0.0 slice-done.1
  692.9 0.0 slice-done.2
  692.9 0.0 slice-done.3
  692.9 0.1 slice-done.4
  693.0 7.5 %copy.25 = bf16[2,5120,1024]{2,1,0:T(8,128)(2,1)} copy(bf16[2,5120,1024]{2,1,0:T(8,128)(2,1)S(1)} %bitcast.13) | data formatting | bytes 41943040
  (2 shorter events, 0.0 us)
Async XLA Ops:
  653.1 4.2 copy-start
  653.1 4.2 copy-start.1
  653.2 4.2 copy-start.2
  653.2 4.2 copy-start.3
  653.2 4.2 copy-start.4
  657.4 25.4 %slice-start.5 = ((s8[20971520]{0:T(1024)(128)(4,1)}), s8[4194304]{0:T(1024)(128)(4,1)S(1)}, s32[]{:S(2)}) async-start(s8[20971520]{0:T(1024)(128)(4,1)} %bitcast.14), calls=%async_computation.5 | async-start | bytes 8388608
  657.4 25.4 %slice-start.6 = ((s8[20971520]{0:T(1024)(128)(4,1)}), s8[4194304]{0:T(1024)(128)(4,1)S(1)}, s32[]{:S(2)}) async-start(s8[20971520]{0:T(1024)(128)(4,1)} %bitcast.14), calls=%async_computation.6 | async-start | bytes 8388608
  661.6 21.3 %slice-start.7 = ((s8[20971520]{0:T(1024)(128)(4,1)}), s8[4194304]{0:T(1024)(128)(4,1)S(1)}, s32[]{:S(2)}) async-start(s8[20971520]{0:T(1024)(128)(4,1)} %bitcast.14), calls=%async_computation.7 | async-start | bytes 8388608
  661.6 21.3 %slice-start.8 = ((s8[20971520]{0:T(1024)(128)(4,1)}), s8[4194304]{0:T(1024)(128)(4,1)S(1)}, s32[]{:S(2)}) async-start(s8[20971520]{0:T(1024)(128)(4,1)} %bitcast.14), calls=%async_computation.8 | async-start | bytes 8388608
  661.6 21.3 %slice-start.9 = ((s8[20971520]{0:T(1024)(128)(4,1)}), s8[4194304]{0:T(1024)(128)(4,1)S(1)}, s32[]{:S(2)}) async-start(s8[20971520]{0:T(1024)(128)(4,1)} %bitcast.14), calls=%async_computation.9 | async-start | bytes 8388608
  661.6 31.4 %slice-start = ((s8[20971520]{0:T(1024)(128)(4,1)}), s8[4194304]{0:T(1024)(128)(4,1)S(1)}, s32[]{:S(2)}) async-start(s8[20971520]{0:T(1024)(128)(4,1)} %bitcast.11), calls=%async_computation | async-start | bytes 8388608
  661.6 31.4 %slice-start.1 = ((s8[20971520]{0:T(1024)(128)(4,1)}), s8[4194304]{0:T(1024)(128)(4,1)S(1)}, s32[]{:S(2)}) async-start(s8[20971520]{0:T(1024)(128)(4,1)} %bitcast.11), calls=%async_computation.1 | async-start | bytes 8388608
  661.6 31.3 %slice-start.2 = ((s8[20971520]{0:T(1024)(128)(4,1)}), s8[4194304]{0:T(1024)(128)(4,1)S(1)}, s32[]{:S(2)}) async-start(s8[20971520]{0:T(1024)(128)(4,1)} %bitcast.11), calls=%async_computation.2 | async-start | bytes 8388608
  682.9 10.1 %slice-start.3 = ((s8[20971520]{0:T(1024)(128)(4,1)}), s8[4194304]{0:T(1024)(128)(4,1)S(1)}, s32[]{:S(2)}) async-start(s8[20971520]{0:T(1024)(128)(4,1)} %bitcast.11), calls=%async_computation.3 | async-start | bytes 8388608
  682.9 10.1 %slice-start.4 = ((s8[20971520]{0:T(1024)(128)(4,1)}), s8[4194304]{0:T(1024)(128)(4,1)S(1)}, s32[]{:S(2)}) async-start(s8[20971520]{0:T(1024)(128)(4,1)} %bitcast.11), calls=%async_computation.4 | async-start | bytes 8388608
